TPU v7x, 32 devices: a whole 2x2x4 slice. The times are simulated.
32 devices in a mesh: lon: 8 (over y, x, core), lat: 4 (over z).
Axes of the slice: x: 2, y: 2, z: 4, core: 2. Of those that a mesh axis runs over, the one named last changes fastest.
Arguments:
- air_state: bfloat16 [4, 24, 192, 192], P(None, 'lat', 'lon'), may hold values from -6 to 6
- upstream: bfloat16 [4, 24, 192, 192], P(None, 'lat', 'lon'), may hold values from -6 to 6
- norm_gain: float32 [192], replicated, may hold values from 0.25 to 1.75
- w_qkv: bfloat16 [192, 576], replicated, may hold values from -0.4375 to 0.4375
- w_proj: bfloat16 [192, 192], replicated, may hold values from -0.4375 to 0.4375
- bias_table: float32 [4, 2, 6, 3312], P('lat'), may hold values from -5 to 260
Outputs:
- block_out: bfloat16 [4, 24, 192, 192], P(None, 'lat', 'lon')
- d_state: bfloat16 [4, 24, 192, 192], P(None, 'lat', 'lon')
- d_gain: float32 [192], replicated
- d_wqkv: float32 [192, 576], replicated
- d_wproj: float32 [192, 192], replicated
- d_table: float32 [4, 2, 6, 3312], P('lat')
All inputs are finite; a program needn't handle non-finite values.
Results may differ from a plain program's by a relative error of at most 0.019.
Values may be sent and summed in bfloat16 or wider, within the bound.
A program may use at most 128 MiB of HBM per device.

v0:
```python
from functools import partial

import jax
import jax.numpy as jnp
from jax import lax
from jax.sharding import PartitionSpec as P

HEADS = 6
WLEV = 2
WLAT = 6
WLON = 12
WIN = 144


epsilon = 1e-05
masked_score = -1000000000.0


def from_behind(array, axis, by):
    peers = lax.axis_size(axis)
    return lax.ppermute(array, axis, [(i, (i + by) % peers) for i in range(peers)])


def layer_norm(as_input, gain_vec):
    average = jnp.mean(as_input, axis=-1, keepdims=True)
    centred = as_input - average
    variance = jnp.mean(centred * centred, axis=-1, keepdims=True)
    return centred * lax.rsqrt(variance + epsilon) * gain_vec


def attention_core(qkv_rows, table_row, first_row, lat_total):
    lev_count, col_count = (qkv_rows.shape[0], qkv_rows.shape[2])
    head_width = qkv_rows.shape[5]
    lev_wins, lon_wins = (lev_count // WLEV, col_count // WLON)
    windowed = qkv_rows.reshape(lev_wins, WLEV, WLAT, lon_wins, WLON, 3, HEADS, head_width)
    windowed = windowed.transpose(5, 0, 3, 6, 1, 2, 4, 7).reshape(
        3, lev_wins, lon_wins, HEADS, WIN, head_width
    )
    queries, keyset, values = (windowed[0], windowed[1], windowed[2])
    scores = jnp.einsum(
        "achid,achjd->achij", queries, keyset, preferred_element_type=jnp.float32
    ) * head_width ** (-0.5)
    picked = table_row.reshape(lev_wins, HEADS, WLEV * WLAT, WLEV * WLAT, 2 * WLON - 1)
    offsets = jnp.arange(WLON)
    onehot = (
        offsets[None, :, None] - offsets[:, None, None] + WLON - 1
        == jnp.arange(2 * WLON - 1)[None, None, :]
    ).astype(jnp.float32)
    expanded = jnp.einsum("ahpqr,ijr->ahpiqj", picked, onehot, precision=lax.Precision.HIGHEST)
    expanded = expanded.reshape(lev_wins, 1, HEADS, WIN, WIN)
    scores = scores + expanded
    lev_index = jnp.arange(lev_wins * WLEV).reshape(lev_wins, WLEV)
    lev_part = (lev_index >= lev_count - WLEV // 2).astype(jnp.int32)
    lat_index = first_row + jnp.arange(WLAT, dtype=jnp.int32)
    lat_part = (lat_index >= lat_total - WLAT // 2).astype(jnp.int32)
    region = (
        2 * lev_part[:, :, None, None]
        + lat_part[None, None, :, None]
        + jnp.zeros((1, 1, 1, WLON), jnp.int32)
    )
    region = region.reshape(lev_wins, WIN)
    same_region = region[:, None, None, :, None] == region[:, None, None, None, :]
    scores = jnp.where(same_region, scores, masked_score)
    row_max = lax.stop_gradient(jnp.max(scores, axis=-1, keepdims=True))
    weights = jnp.exp(scores - row_max)
    softened = (weights / jnp.sum(weights, axis=-1, keepdims=True)).astype(jnp.bfloat16)
    mixture = jnp.einsum(
        "achij,achjd->achid", softened, values, preferred_element_type=jnp.float32
    ).astype(jnp.bfloat16)
    mixture = mixture.reshape(lev_wins, lon_wins, HEADS, WLEV, WLAT, WLON, head_width)
    return mixture.transpose(0, 3, 4, 1, 5, 2, 6).reshape(
        lev_count, WLAT, col_count, HEADS * head_width
    )


def local_sublayer(shifted, shifted_up, gain_vec, w_qkv, w_proj, table_row, first_row, lat_total):
    lev_count, row_count, col_count, width = shifted.shape
    pre_norm, norm_back = jax.vjp(layer_norm, shifted.astype(jnp.float32), gain_vec)
    normed = pre_norm.astype(jnp.bfloat16).reshape(-1, width)
    qkv_rows = jnp.dot(normed, w_qkv, preferred_element_type=jnp.float32).astype(jnp.bfloat16)
    qkv_rows = qkv_rows.reshape(lev_count, row_count, col_count, 3, HEADS, width // HEADS)
    core_fn = partial(attention_core, first_row=first_row, lat_total=lat_total)
    mixture, core_back = jax.vjp(core_fn, qkv_rows, table_row)
    flat_rows = mixture.reshape(-1, width)
    branch = jnp.dot(flat_rows, w_proj, preferred_element_type=jnp.float32).astype(jnp.bfloat16)
    up_rows = shifted_up.reshape(-1, width)
    d_proj = jnp.einsum("ti,to->io", flat_rows, up_rows, preferred_element_type=jnp.float32)
    d_mixed = jnp.einsum("to,io->ti", up_rows, w_proj, preferred_element_type=jnp.float32).astype(
        jnp.bfloat16
    )
    d_qkv, d_row = core_back(d_mixed.reshape(mixture.shape))
    d_qkv = d_qkv.reshape(-1, 3 * width)
    d_wqkv = jnp.einsum("ti,to->io", normed, d_qkv, preferred_element_type=jnp.float32)
    d_normed = jnp.einsum("to,io->ti", d_qkv, w_qkv, preferred_element_type=jnp.float32)
    d_input, d_gain = norm_back(d_normed.reshape(lev_count, row_count, col_count, width))
    branch = branch.reshape(lev_count, row_count, col_count, width)
    return (branch, d_input.astype(jnp.bfloat16), d_gain, d_wqkv, d_proj, d_row)


def on_device(air_state, upstream, norm_gain, w_qkv, w_proj, bias_table):
    lev_shift, lat_shift, lon_shift = (WLEV // 2, WLAT // 2, WLON // 2)
    lon_edge = from_behind((air_state[:, :, :lon_shift], upstream[:, :, :lon_shift]), "lon", -1)
    shifted = jnp.concatenate([air_state[:, :, lon_shift:], lon_edge[0]], axis=2)
    shifted_up = jnp.concatenate([upstream[:, :, lon_shift:], lon_edge[1]], axis=2)
    lat_rim = from_behind((shifted[:, :lat_shift], shifted_up[:, :lat_shift]), "lat", -1)
    shifted = jnp.roll(jnp.concatenate([shifted[:, lat_shift:], lat_rim[0]], axis=1), -lev_shift, 0)
    shifted_up = jnp.roll(
        jnp.concatenate([shifted_up[:, lat_shift:], lat_rim[1]], axis=1), -lev_shift, 0
    )
    row_count = air_state.shape[1]
    width = air_state.shape[3]
    row_base = lax.axis_index("lat") * row_count
    lat_total = lax.axis_size("lat") * row_count

    def row_step(totals, window_row):
        first_local = window_row * WLAT
        table_row = lax.dynamic_index_in_dim(bias_table, window_row, 0, keepdims=False)
        results = local_sublayer(
            shifted,
            shifted_up,
            norm_gain,
            w_qkv,
            w_proj,
            table_row,
            row_base + first_local,
            lat_total,
        )
        totals = tuple((before + added for before, added in zip(totals, results[2:5])))
        return (totals, (results[0], results[1], results[5]))

    zeros_init = (
        jnp.zeros((width,), jnp.float32),
        jnp.zeros((width, 3 * width), jnp.float32),
        jnp.zeros((width, width), jnp.float32),
    )
    totals, (branch, d_input, d_band) = lax.scan(
        row_step, zeros_init, jnp.arange(row_count // WLAT, dtype=jnp.int32)
    )
    d_gain, d_wqkv, d_proj = totals
    shape_in = air_state.shape
    branch = jnp.roll(branch.transpose(1, 0, 2, 3, 4).reshape(shape_in), lev_shift, 0)
    d_input = jnp.roll(d_input.transpose(1, 0, 2, 3, 4).reshape(shape_in), lev_shift, 0)
    lat_rim = from_behind((branch[:, -lat_shift:], d_input[:, -lat_shift:]), "lat", 1)
    branch = jnp.concatenate([lat_rim[0], branch[:, :-lat_shift]], axis=1)
    d_input = jnp.concatenate([lat_rim[1], d_input[:, :-lat_shift]], axis=1)
    lon_edge = from_behind((branch[:, :, -lon_shift:], d_input[:, :, -lon_shift:]), "lon", 1)
    branch = jnp.concatenate([lon_edge[0], branch[:, :, :-lon_shift]], axis=2)
    d_input = jnp.concatenate([lon_edge[1], d_input[:, :, :-lon_shift]], axis=2)
    block_out = (air_state.astype(jnp.float32) + branch.astype(jnp.float32)).astype(jnp.bfloat16)
    d_state = (upstream.astype(jnp.float32) + d_input.astype(jnp.float32)).astype(jnp.bfloat16)
    d_gain, d_wqkv, d_proj, d_table = (
        lax.psum(d_gain.astype(jnp.bfloat16), "lon").astype(jnp.float32),
        lax.psum(d_wqkv.astype(jnp.bfloat16), "lon").astype(jnp.float32),
        lax.psum(d_proj.astype(jnp.bfloat16), "lon").astype(jnp.float32),
        lax.psum(d_band.astype(jnp.bfloat16), "lon").astype(jnp.float32),
    )
    d_gain, d_wqkv, d_proj = (
        lax.psum(d_gain.astype(jnp.bfloat16), "lat").astype(jnp.float32),
        lax.psum(d_wqkv.astype(jnp.bfloat16), "lat").astype(jnp.float32),
        lax.psum(d_proj.astype(jnp.bfloat16), "lat").astype(jnp.float32),
    )
    return (block_out, d_state, d_gain, d_wqkv, d_proj, d_table)


def solution(mesh):
    return jax.shard_map(
        on_device,
        mesh=mesh,
        in_specs=(
            P(None, "lat", "lon", None),
            P(None, "lat", "lon", None),
            P(),
            P(),
            P(),
            P("lat", None, None, None),
        ),
        out_specs=(
            P(None, "lat", "lon", None),
            P(None, "lat", "lon", None),
            P(),
            P(),
            P(),
            P("lat", None, None, None),
        ),
        check_vma=False,
    )
```

profile of v0, /device:TPU:0, one launch (start us, length us, event | category | flops | bytes accessed | tf_op | source)
XLA Modules:
  0.0 286.9 jit_solution(3721767121218056231)
XLA Ops:
  8.2 3.4 %collective-permute-start.4 = (bf16[4,6,6,192]{3,2,1,0:T(8,128)(2,1)S(1)}, bf16[4,6,6,192]{3,2,1,0:T(8,128)(2,1)S(1)}, u32[]{:S(2)}, u32[]{:S(2)}) collective-permute-start(bf16[4,6,6,192]{3,2,1,0:T(8,128)(2,1)S(1)} %slice.116), channel_id=1, source_target_pairs={{0,28},{4,0},{8,4},{12,8},{16,12},{20,16},{24,20},{28,24},{1,29},{... | collective-permute-start | bytes 165896 | tf_op jit(solution)/shard_map/ppermute | solution.py:21
  13.4 1.8 reshape.288
  15.2 8.8 %convolution_bitcast_fusion = f32[2,6,12,12,12,12]{4,5,2,1,0,3:T(8,128)} fusion(f32[2,6,12,12,23]{4,3,2,0,1:T(8,128)S(1)} %reshape.288, s32[12,12]{1,0:T(8,128)S(1)} %subtract_add_fusion), kind=kOutput, calls=%fused_computation.3 | convolution fusion | flops 68680944 | bytes 1154880 | tf_op jit(solution)/shard_map/while/body/eval_jaxpr/jvp(ahpqr,ijr->ahpiqj)/dot_general | solution.py:49
  24.3 21.3 %copy.90 = f32[2,6,12,12,12,12]{3,2,5,4,1,0:T(8,128)} copy(f32[2,6,12,12,12,12]{4,5,2,1,0,3:T(8,128)} %convolution_bitcast_fusion) | data formatting | bytes 1990656 | tf_op jit(solution)/shard_map/while/body/eval_jaxpr/jvp()/add | solution.py:51
  45.6 10.2 %reshape.302 = f32[2,6,144,144]{2,3,1,0:T(8,128)} reshape(f32[2,6,12,12,12,12]{3,2,5,4,1,0:T(8,128)} %copy.90) | data formatting | bytes 1990656 | tf_op jit(solution)/shard_map/while/body/eval_jaxpr/jvp()/add | solution.py:51
  55.9 3.7 %collective-permute-start.1 = (bf16[4,3,24,192]{3,2,1,0:T(8,128)(2,1)S(1)}, bf16[4,3,24,192]{3,2,1,0:T(8,128)(2,1)S(1)}, u32[]{:S(2)}, u32[]{:S(2)}) collective-permute-start(bf16[4,3,24,192]{3,2,1,0:T(8,128)(2,1)S(1)} %get-tuple-element.65), channel_id=1, source_target_pairs={{0,3},{1,0},{2,1},{3,2},{4,7},{5,4},{6,5},{7,6},{8,11},{9,8},{10,9... | collective-permute-start | bytes 331784 | tf_op jit(solution)/shard_map/ppermute | solution.py:21
  60.2 3.6 %collective-permute-done.1 = bf16[4,3,24,192]{3,2,1,0:T(8,128)(2,1)S(1)} collective-permute-done((bf16[4,3,24,192]{3,2,1,0:T(8,128)(2,1)S(1)}, bf16[4,3,24,192]{3,2,1,0:T(8,128)(2,1)S(1)}, u32[]{:S(2)}, u32[]{:S(2)}) %collective-permute-start.1) | collective-permute-done | bytes 110624 | tf_op jit(solution)/shard_map/ppermute | solution.py:21
  69.9 3.9 %reshape.287 = bf16[2,2,6,2,12,3,6,32]{7,6,5,4,3,2,1,0:T(8,128)(2,1)} reshape(bf16[576,576]{1,0:T(8,128)(2,1)S(1)} %convolution_convert_fusion.1) | data formatting | bytes 1327104 | tf_op jit(solution)/shard_map/while/body/eval_jaxpr/jvp()/reshape;while/body/eval_jaxpr/reshape | solution.py:35
  73.8 3.0 %fusion.73 = (bf16[1,2,2,6,2,6,12,32]{7,3,0,6,2,5,4,1:T(8,128)(2,1)S(1)}, bf16[1,2,2,6,2,6,12,32]{7,3,0,6,2,5,4,1:T(8,128)(2,1)S(1)}, bf16[1,2,2,6,2,6,12,32]{7,3,0,6,2,5,4,1:T(8,128)(2,1)S(1)}) fusion(bf16[3,2,2,6,2,6,12,32]{7,3,0,6,2,5,4,1:T(8,128)(2,1)} %bitcast.90), kind=kLoop, calls=%fused_computation.113 | loop fusion | bytes 1327104 | tf_op jit(solution)/shard_map/while/body/eval_jaxpr/jvp()/slice | solution.py:39
  78.4 3.0 %copy.56 = bf16[2,2,6,144,32]{3,4,2,1,0:T(8,128)(2,1)} copy(bf16[2,2,6,144,32]{4,1,3,2,0:T(2,128)(2,1)} %bitcast.94) | data formatting | bytes 442368 | tf_op jit(solution)/shard_map/while/body/eval_jaxpr/jvp()/squeeze | solution.py:39
  83.1 2.4 copy.62
  87.0 2.3 copy.55
  89.4 4.7 %fusion.74 = (f32[2,2,6,144]{3,2,1,0:T(8,128)S(1)}, f32[2,2,6,144,144]{3,4,2,1,0:T(8,128)}) fusion(f32[2,6,144,144]{2,3,1,0:T(8,128)} %reshape.302, pred[2,144,144]{1,2,0:T(8,128)(4,1)S(1)} %broadcast_compare_fusion, bf16[2,2,6,144,32]{3,4,2,1,0:T(8,128)(2,1)S(1)} %copy.55, bf16[2,2,6,144,32]{3,4,2,1,0:T(8,128)(2,1)S(1)} %copy-done.13), kind=kOutput, calls=%fused_computation.114 | convolution fusion | flops 34338960 | bytes 3483648 | tf_op jit(solution)/shard_map/while/body/eval_jaxpr/jvp()/sub | solution.py:65
  94.1 3.0 %fusion.7 = (f32[2,2,6,144]{3,2,1,0:T(8,128)S(1)}, bf16[2,2,6,144,144]{3,4,2,1,0:T(8,128)(2,1)S(1)}) fusion(f32[2,2,6,144,144]{3,4,2,1,0:T(8,128)} %get-tuple-element.68, f32[2,2,6,144]{3,2,1,0:T(8,128)S(1)} %multiply_divide_fusion, bf16[2,2,6,144,32]{3,4,2,1,0:T(8,128)(2,1)S(1)} %copy.70, bf16[2,2,6,144,32]{3,4,2,1,0:T(8,128)(2,1)S(1)} %copy.62), kind=kOutput, calls=%fused_computation.10 | convolution fusion | flops 34335360 | bytes 3456000 | tf_op jit(solution)/shard_map/while/body/eval_jaxpr/transpose(jvp(achij,achjd->achid))/dot_general | solution.py:67
  97.2 1.8 fusion.31
  99.0 1.9 fusion.34
  100.8 2.4 fusion.70
  108.4 2.4 pad_add_fusion
  110.8 5.7 %copy.77 = bf16[3,2,2,6,144,32]{5,2,4,3,1,0:T(2,128)(2,1)S(1)} copy(bf16[3,2,2,6,144,32]{4,5,3,2,1,0:T(8,128)(2,1)} %pad_add_fusion) | data formatting | bytes 1327104 | tf_op jit(solution)/shard_map/while/body/eval_jaxpr/transpose(jvp())/add_any | solution.py:39
  116.5 2.9 %copy.78 = bf16[2,2,6,2,12,3,6,32]{7,6,5,4,3,2,1,0:T(8,128)(2,1)} copy(bf16[2,2,6,2,12,3,6,32]{7,3,4,2,1,6,0,5:T(2,128)(2,1)S(1)} %bitcast.91) | data formatting | bytes 1327104 | tf_op jit(solution)/shard_map/while/body/eval_jaxpr/transpose(jvp())/transpose | solution.py:36
  119.4 4.1 %reshape.295 = bf16[576,576]{1,0:T(8,128)(2,1)S(1)} reshape(bf16[2,2,6,2,12,3,6,32]{7,6,5,4,3,2,1,0:T(8,128)(2,1)} %copy.78) | data formatting | bytes 1327104 | tf_op jit(solution)/shard_map/while/body/eval_jaxpr/reshape;while/body/eval_jaxpr/transpose(jvp())/reshape | solution.py:92
  123.5 4.9 %dot_general.68 = bf16[4,6,24,576]{3,2,1,0:T(8,128)(2,1)} reshape(bf16[2,2,6,2,12,3,6,32]{7,6,5,4,3,2,1,0:T(8,128)(2,1)} %copy.78) | data formatting | bytes 1327104 | tf_op jit(solution)/shard_map/while/body/eval_jaxpr/to,io->ti/dot_general | solution.py:94
  128.4 1.7 multiply_reduce_fusion.1
  131.7 2.0 copy.80
  135.1 11.8 %psum.49 = bf16[192]{0:T(256)(128)(2,1)S(1)} all-reduce(bf16[192]{0:T(256)(128)(2,1)S(1)} %get-tuple-element.34), channel_id=1, replica_groups=mesh['lon'=8,'lat'=4] {'lon'}, use_global_device_ids=true, to_apply=%region_8.9 | all-reduce | flops 192 | bytes 768 | tf_op jit(solution)/shard_map/psum | solution.py:152
  146.9 12.2 %psum.50 = bf16[192]{0:T(256)(128)(2,1)S(1)} all-reduce(bf16[192]{0:T(256)(128)(2,1)S(1)} %psum.49), channel_id=1, replica_groups=mesh['lon'=8,'lat'=4] {'lat'}, use_global_device_ids=true, to_apply=%region_9.10 | all-reduce | flops 192 | bytes 768 | tf_op jit(solution)/shard_map/psum | solution.py:158
  160.5 10.1 %reshape.296 = f32[2,6,12,12,12,12]{5,4,3,2,1,0:T(8,128)} reshape(f32[2,6,144,144]{3,2,1,0:T(8,128)} %copy.80) | data formatting | bytes 1990656 | tf_op jit(solution)/shard_map/while/body/eval_jaxpr/transpose(jvp())/reshape;while/body/eval_jaxpr/transpose(jvp())/reshape | solution.py:50
  170.6 10.8 %fusion.22 = bf16[2,6,12,12,23]{4,3,2,1,0:T(8,128)(2,1)S(1)} fusion(f32[2,6,12,12,12,12]{5,4,3,2,1,0:T(8,128)} %reshape.296, s32[12,12]{1,0:T(8,128)S(1)} %copy-done.17), kind=kOutput, calls=%fused_computation.28 | convolution fusion | flops 68720688 | bytes 1075392 | tf_op jit(solution)/shard_map/while/body/eval_jaxpr/transpose(jvp(ahpqr,ijr->ahpiqj))/dot_general | solution.py:49
  184.2 53.5 %all-reduce.8.cloned.1.call-done = (bf16[192,576]{1,0:T(8,128)(2,1)}, bf16[192,192]{1,0:T(8,128)(2,1)}, bf16[1,2,6,3312]{3,1,2,0:T(2,128)(2,1)}) async-done(((bf16[192,576]{1,0:T(8,128)(2,1)}, bf16[192,192]{1,0:T(8,128)(2,1)}, bf16[1,2,6,3312]{3,1,2,0:T(2,128)(2,1)}), (bf16[192,576]{1,0:T(8,128)(2,1)}, bf16[192,192]{1,0:T(8,128)(2,1)}, bf16[1,2,6,3312]{3,1,2,0:T(2,128)(2,1)})) %all-reduce.8.cloned.1.call-update) | async-done | bytes 374416 | tf_op jit(solution)/shard_map/psum | solution.py:153
  239.5 1.6 convert_element_type.183
  241.1 35.7 %all-reduce.10.cloned.1.call-done = (bf16[192,576]{1,0:T(8,128)(2,1)}, bf16[192,192]{1,0:T(8,128)(2,1)}) async-done(((bf16[192,576]{1,0:T(8,128)(2,1)}, bf16[192,192]{1,0:T(8,128)(2,1)}), (bf16[192,576]{1,0:T(8,128)(2,1)}, bf16[192,192]{1,0:T(8,128)(2,1)})) %all-reduce.10.cloned.1.call-update) | async-done | bytes 294928 | tf_op jit(solution)/shard_map/psum | solution.py:159
  278.3 1.8 convert_element_type.178
  (126 shorter events, 30.0 us)
Async XLA Ops:
  7.2 62.3 %copy-start = (bf16[192,576]{1,0:T(8,128)(2,1)S(1)}, bf16[192,576]{1,0:T(8,128)(2,1)}, u32[]{:S(2)}) copy-start(bf16[192,576]{1,0:T(8,128)(2,1)} %param.9) | copy-start | bytes 663556
  7.2 230.5 %all-reduce.8.cloned.1.call-start = ((), (), s32[]{:S(2)}) async-start(), calls=%async_computation | async-start | bytes 847872 | tf_op jit(solution)/shard_map/psum | solution.py:153
  8.2 51.4 %collective-permute-start.4 = (bf16[4,6,6,192]{3,2,1,0:T(8,128)(2,1)S(1)}, bf16[4,6,6,192]{3,2,1,0:T(8,128)(2,1)S(1)}, u32[]{:S(2)}, u32[]{:S(2)}) collective-permute-start(bf16[4,6,6,192]{3,2,1,0:T(8,128)(2,1)S(1)} %slice.116), channel_id=1, source_target_pairs={{0,28},{4,0},{8,4},{12,8},{16,12},{20,16},{24,20},{28,24},{1,29},{... | collective-permute-start | bytes 165896 | tf_op jit(solution)/shard_map/ppermute | solution.py:21
  12.5 43.4 %collective-permute-start = (bf16[4,6,6,192]{3,2,1,0:T(8,128)(2,1)S(1)}, bf16[4,6,6,192]{3,2,1,0:T(8,128)(2,1)S(1)}, u32[]{:S(2)}, u32[]{:S(2)}) collective-permute-start(bf16[4,6,6,192]{3,2,1,0:T(8,128)(2,1)S(1)} %slice.99), channel_id=1, source_target_pairs={{0,28},{4,0},{8,4},{12,8},{16,12},{20,16},{24,20},{28,24},{1,29},{... | collective-permute-start | bytes 165896 | tf_op jit(solution)/shard_map/ppermute | solution.py:21
  13.1 10.8 %copy-start.16 = (s32[12,12]{1,0:T(8,128)}, s32[12,12]{1,0:T(8,128)S(1)}, u32[]{:S(2)}) copy-start(s32[12,12]{1,0:T(8,128)S(1)} %subtract_add_fusion) | copy-start | bytes 1732
  15.2 8.9 %copy-start.3 = (bf16[4,6,24,192]{3,2,1,0:T(8,128)(2,1)S(1)}, bf16[4,6,24,192]{3,2,1,0:T(8,128)(2,1)}, u32[]{:S(2)}) copy-start(bf16[4,6,24,192]{3,2,1,0:T(8,128)(2,1)} %param.6) | copy-start | bytes 663556
  15.2 9.0 %copy-start.5 = (bf16[4,6,24,192]{3,2,1,0:T(8,128)(2,1)S(1)}, bf16[4,6,24,192]{3,2,1,0:T(8,128)(2,1)}, u32[]{:S(2)}) copy-start(bf16[4,6,24,192]{3,2,1,0:T(8,128)(2,1)} %param.7) | copy-start | bytes 663556
  55.8 10.9 %copy-start.12 = (bf16[192,192]{1,0:T(8,128)(2,1)S(1)}, bf16[192,192]{1,0:T(8,128)(2,1)}, u32[]{:S(2)}) copy-start(bf16[192,192]{1,0:T(8,128)(2,1)} %param.10) | copy-start | bytes 221188
  55.9 7.9 %collective-permute-start.1 = (bf16[4,3,24,192]{3,2,1,0:T(8,128)(2,1)S(1)}, bf16[4,3,24,192]{3,2,1,0:T(8,128)(2,1)S(1)}, u32[]{:S(2)}, u32[]{:S(2)}) collective-permute-start(bf16[4,3,24,192]{3,2,1,0:T(8,128)(2,1)S(1)} %get-tuple-element.65), channel_id=1, source_target_pairs={{0,3},{1,0},{2,1},{3,2},{4,7},{5,4},{6,5},{7,6},{8,11},{9,8},{10,9... | collective-permute-start | bytes 331784 | tf_op jit(solution)/shard_map/ppermute | solution.py:21
  59.7 6.2 %collective-permute-start.5 = (bf16[4,3,24,192]{3,2,1,0:T(8,128)(2,1)S(1)}, bf16[4,3,24,192]{3,2,1,0:T(8,128)(2,1)S(1)}, u32[]{:S(2)}, u32[]{:S(2)}) collective-permute-start(bf16[4,3,24,192]{3,2,1,0:T(8,128)(2,1)S(1)} %get-tuple-element.63), channel_id=1, source_target_pairs={{0,3},{1,0},{2,1},{3,2},{4,7},{5,4},{6,5},{7,6},{8,11},{9,8},{10,9... | collective-permute-start | bytes 331784 | tf_op jit(solution)/shard_map/ppermute | solution.py:21
  64.3 4.9 %copy-start.18 = (f32[4,6,24]{2,1,0:T(8,128)}, f32[4,6,24]{2,1,0:T(8,128)S(1)}, u32[]{:S(2)}) copy-start(f32[4,6,24]{2,1,0:T(8,128)S(1)} %multiply_reduce_fusion.2) | copy-start | bytes 6916
  64.4 4.9 %copy-start.14 = (f32[4,6,24]{2,1,0:T(8,128)}, f32[4,6,24]{2,1,0:T(8,128)S(1)}, u32[]{:S(2)}) copy-start(f32[4,6,24]{2,1,0:T(8,128)S(1)} %fusion.64) | copy-start | bytes 6916
  65.9 3.4 %copy-start.20 = (f32[192]{0:T(256)S(1)}, f32[192]{0:T(256)}, u32[]{:S(2)}) copy-start(f32[192]{0:T(256)} %param.8) | copy-start | bytes 2308
  83.1 6.3 %copy-start.13 = (bf16[2,2,6,144,32]{3,4,2,1,0:T(8,128)(2,1)S(1)}, bf16[2,2,6,144,32]{3,4,2,1,0:T(8,128)(2,1)}, u32[]{:S(2)}) copy-start(bf16[2,2,6,144,32]{3,4,2,1,0:T(8,128)(2,1)} %copy.56) | copy-start | bytes 663556
  94.1 3.1 %copy-start.1 = (f32[2,2,6,144,144]{3,4,2,1,0:T(8,128)S(1)}, f32[2,2,6,144,144]{3,4,2,1,0:T(8,128)}, u32[]{:S(2)}) copy-start(f32[2,2,6,144,144]{3,4,2,1,0:T(8,128)} %get-tuple-element.68) | copy-start | bytes 5971972
  105.0 3.4 %copy-start.7 = (bf16[1,2,2,6,144,32]{4,5,3,2,1,0:T(8,128)(2,1)S(1)}, bf16[1,2,2,6,144,32]{4,5,3,2,1,0:T(8,128)(2,1)}, u32[]{:S(2)}) copy-start(bf16[1,2,2,6,144,32]{4,5,3,2,1,0:T(8,128)(2,1)} %fusion.37) | copy-start | bytes 663556
  108.2 11.1 %copy-start.8 = (bf16[576,192]{0,1:T(8,128)(2,1)}, bf16[576,192]{0,1:T(8,128)(2,1)S(1)}, u32[]{:S(2)}) copy-start(bf16[576,192]{0,1:T(8,128)(2,1)S(1)} %convolution_convert_fusion.5) | copy-start | bytes 663556
  119.4 9.0 %copy-start.21 = (f32[192]{0:T(256)S(1)}, f32[192]{0:T(256)}, u32[]{:S(2)}) copy-start(f32[192]{0:T(256)} %param.8) | copy-start | bytes 2308
  123.5 6.7 %copy-start.19 = (f32[4,6,24]{2,1,0:T(8,128)S(1)}, f32[4,6,24]{2,1,0:T(8,128)}, u32[]{:S(2)}) copy-start(f32[4,6,24]{2,1,0:T(8,128)} %copy-done.18) | copy-start | bytes 6916
  123.5 6.7 %copy-start.15 = (f32[4,6,24]{2,1,0:T(8,128)S(1)}, f32[4,6,24]{2,1,0:T(8,128)}, u32[]{:S(2)}) copy-start(f32[4,6,24]{2,1,0:T(8,128)} %copy-done.14) | copy-start | bytes 6916
  123.5 6.7 %copy-start.22 = (f32[192]{0:T(256)S(1)}, f32[192]{0:T(256)}, u32[]{:S(2)}) copy-start(f32[192]{0:T(256)} %param.8) | copy-start | bytes 2308
  128.4 3.3 %copy-start.2 = (f32[2,6,144,144]{2,3,1,0:T(8,128)S(1)}, f32[2,6,144,144]{2,3,1,0:T(8,128)}, u32[]{:S(2)}) copy-start(f32[2,6,144,144]{2,3,1,0:T(8,128)} %get-tuple-element.57) | copy-start | bytes 2985988
  130.1 3.7 %slice-start = ((bf16[576,192]{0,1:T(8,128)(2,1)}), bf16[432,192]{0,1:T(8,128)(2,1)S(1)}, s32[]{:S(2)}) async-start(bf16[576,192]{0,1:T(8,128)(2,1)} %copy-done.8), calls=%async_computation.2 | async-start | bytes 393216 | tf_op jit(solution)/shard_map/jit(_roll_static)/slice | solution.py:141
  134.6 49.3 %collective-permute-start.2 = (bf16[4,3,24,192]{3,2,1,0:T(8,128)(2,1)}, bf16[4,3,24,192]{3,2,1,0:T(8,128)(2,1)S(1)}, u32[]{:S(2)}, u32[]{:S(2)}) collective-permute-start(bf16[4,3,24,192]{3,2,1,0:T(8,128)(2,1)} %fusion.56), channel_id=1, source_target_pairs={{0,1},{1,2},{2,3},{3,0},{4,5},{5,6},{6,7},{7,4},{8,9},{9,10},{10,1... | collective-permute-start | bytes 331784 | tf_op jit(solution)/shard_map/ppermute | solution.py:21
  160.3 10.3 %copy-start.17 = (s32[12,12]{1,0:T(8,128)S(1)}, s32[12,12]{1,0:T(8,128)}, u32[]{:S(2)}) copy-start(s32[12,12]{1,0:T(8,128)} %copy-done.16) | copy-start | bytes 1732
  160.3 23.7 %collective-permute-start.6 = (bf16[4,3,24,192]{3,2,1,0:T(8,128)(2,1)}, bf16[4,3,24,192]{3,2,1,0:T(8,128)(2,1)S(1)}, u32[]{:S(2)}, u32[]{:S(2)}) collective-permute-start(bf16[4,3,24,192]{3,2,1,0:T(8,128)(2,1)} %fusion.54), channel_id=1, source_target_pairs={{0,1},{1,2},{2,3},{3,0},{4,5},{5,6},{6,7},{7,4},{8,9},{9,10},{10,1... | collective-permute-start | bytes 331784 | tf_op jit(solution)/shard_map/ppermute | solution.py:21
  170.6 10.8 %copy-start.11 = (bf16[4,6,24,192]{3,2,1,0:T(8,128)(2,1)S(1)}, bf16[4,6,24,192]{3,2,1,0:T(8,128)(2,1)}, u32[]{:S(2)}) copy-start(bf16[4,6,24,192]{3,2,1,0:T(8,128)(2,1)} %get-tuple-element.66) | copy-start | bytes 663556
  181.4 56.3 %copy-start.4 = (bf16[4,6,24,192]{3,2,1,0:T(8,128)(2,1)S(1)}, bf16[4,6,24,192]{3,2,1,0:T(8,128)(2,1)}, u32[]{:S(2)}) copy-start(bf16[4,6,24,192]{3,2,1,0:T(8,128)(2,1)} %param.6) | copy-start | bytes 663556
  181.4 57.2 %copy-start.6 = (bf16[4,6,24,192]{3,2,1,0:T(8,128)(2,1)S(1)}, bf16[4,6,24,192]{3,2,1,0:T(8,128)(2,1)}, u32[]{:S(2)}) copy-start(bf16[4,6,24,192]{3,2,1,0:T(8,128)(2,1)} %param.7) | copy-start | bytes 663556
  183.9 92.9 %all-reduce.10.cloned.1.call-start = ((), (), s32[]{:S(2)}) async-start(), calls=%async_computation.1 | async-start | bytes 688128 | tf_op jit(solution)/shard_map/psum | solution.py:159
  184.0 53.8 %collective-permute-start.3 = (bf16[4,6,6,192]{3,2,1,0:T(8,128)(2,1)S(1)}, bf16[4,6,6,192]{3,2,1,0:T(8,128)(2,1)S(1)}, u32[]{:S(2)}, u32[]{:S(2)}) collective-permute-start(bf16[4,6,6,192]{3,2,1,0:T(8,128)(2,1)S(1)} %pad_maximum_fusion.9), channel_id=1, source_target_pairs={{0,4},{4,8},{8,12},{12,16},{16,20},{20,24},{24,28},{28,0},{1,5},{5... | collective-permute-start | bytes 165896 | tf_op jit(solution)/shard_map/ppermute | solution.py:21
  184.1 54.5 %collective-permute-start.7 = (bf16[4,6,6,192]{3,2,1,0:T(8,128)(2,1)S(1)}, bf16[4,6,6,192]{3,2,1,0:T(8,128)(2,1)S(1)}, u32[]{:S(2)}, u32[]{:S(2)}) collective-permute-start(bf16[4,6,6,192]{3,2,1,0:T(8,128)(2,1)S(1)} %pad_maximum_fusion.8), channel_id=1, source_target_pairs={{0,4},{4,8},{8,12},{12,16},{16,20},{20,24},{24,28},{28,0},{1,5},{5... | collective-permute-start | bytes 165896 | tf_op jit(solution)/shard_map/ppermute | solution.py:21
  (2 other events, 3.1 us)
Sparse Core Ops, SparseCore 0:
  184.0 53.6 all-reduce.7
  240.1 36.5 all-reduce.9
where the time goes:
time: 288 us; the launch traced here: 287 us
  waiting for transfers between devices  94.2 us (33%)
  local copies, waits for them, and re-layouts  91.5 us (32%)
  matrix products  37.4 us (13%)
  blocking collectives  24 us (8%)
  other arithmetic  16.1 us (6%)
  between operations  14.7 us (5%)
  starting transfers between devices  9.02 us (3%)
    psum x1, waiting for transfers between devices, on_device(): lax.psum(d_wqkv.astype(jnp.bfloat16), 'lon').astype(jnp.float32)  53.5 us
    psum x1, waiting for transfers between devices, on_device(): lax.psum(d_wqkv.astype(jnp.bfloat16), 'lat').astype(jnp.float32)  35.7 us
    add x2, local copies, waits for them, and re-layouts, attention_core(): scores = scores + expanded  31.5 us
    dot_general x2, matrix products, attention_core(): jnp.einsum('ahpqr,ijr->ahpiqj', picked, onehot, precision=lax.Precision.H...  19.6 us
    psum x1, blocking collectives, on_device(): lax.psum(d_gain.astype(jnp.bfloat16), 'lat').astype(jnp.float32)  12.2 us
    psum x1, blocking collectives, on_device(): lax.psum(d_gain.astype(jnp.bfloat16), 'lon').astype(jnp.float32)  11.8 us
    reshape x1, local copies, waits for them, and re-layouts, attention_core(): expanded = expanded.reshape(lev_wins, 1, HEADS, WIN, WIN)  10.1 us
    ppermute x8, starting transfers between devices, from_behind(): lax.ppermute(array, axis, [(i, (i + by) % peers) for i in range(peers)])  8.94 us
  transfers between devices with their start and end apart: 10, of which 4 were waited for; matrix products, arithmetic and copies ran while one was open for 25% of the time, Pallas kernels for 0%

commit v1 on v0

v1 whole, which is shorter than its diff:
```python
from functools import partial

import jax
import jax.numpy as jnp
from jax import lax
from jax.experimental import pallas as pl
from jax.experimental.pallas import tpu as pltpu
from jax.sharding import PartitionSpec as P

HEADS = 6
WLEV = 2
WLAT = 6
WLON = 12
WIN = 144
PLACES = WLEV * WLAT
OFFS = 2 * WLON - 1
LAT_SHIFT = WLAT // 2
LON_SHIFT = WLON // 2
EDGE = 8

epsilon = 1e-05
masked_score = -1000000000.0
F32 = jnp.float32
BF16 = jnp.bfloat16


def mm(a, b):
    return lax.dot_general(a, b, (((1,), (0,)), ((), ())), preferred_element_type=F32)


def mm_nt(a, b):
    return lax.dot_general(a, b, (((1,), (1,)), ((), ())), preferred_element_type=F32)


def mm_tn(a, b):
    return lax.dot_general(a, b, (((0,), (0,)), ((), ())), preferred_element_type=F32)


def group_of(n):
    return sum((n >= WLON * m).astype(jnp.int32) for m in range(1, PLACES))


def selection(lon_i):
    k = lax.broadcasted_iota(jnp.int32, (PLACES * OFFS, WIN), 0)
    n = lax.broadcasted_iota(jnp.int32, (1, WIN), 1)
    target = n + (OFFS - WLON) * group_of(n) + (WLON - 1) - lon_i
    return jnp.where(k == target, 1.0, 0.0).astype(BF16)


def core_kernel(
    air, up, east, north, corner, gain, w_qkv, w_proj, table,
    out24, out8, grads, d_table,
    x, y, xhat, rstd_s, normed, qkv, d_mix, bias, d_bias, acc_o, acc_dq, acc_dk, acc_dv, dqkv, mix, stage,
):
    lev, rows, cols, width = air.shape
    lev_wins, lon_wins = lev // WLEV, cols // WLON
    wins = lev_wins * lon_wins
    head_width = width // HEADS
    scale = head_width ** (-0.5)

    for src, (dst) in enumerate((x, y)):
        local = (air, up)[src]
        for rl in range(lev):
            a, l = divmod(rl, WLEV)
            ol = (rl + WLEV // 2) % lev
            for t in range(WLAT):
                p = l * WLAT + t
                if t < WLAT - LAT_SHIFT:
                    row = local[ol, t + LAT_SHIFT].astype(F32)
                    edge = east[src, ol, t + LAT_SHIFT].astype(F32)
                else:
                    row = north[src, ol, t - (WLAT - LAT_SHIFT)].astype(F32)
                    edge = corner[src, ol, t - (WLAT - LAT_SHIFT)].astype(F32)
                for c in range(lon_wins):
                    w = a * lon_wins + c
                    lo = LON_SHIFT + c * WLON
                    if c < lon_wins - 1:
                        dst[w, p * WLON:(p + 1) * WLON, :] = row[lo:lo + WLON]
                    else:
                        dst[w, p * WLON:p * WLON + WLON - LON_SHIFT, :] = row[lo:cols]
                        dst[w, p * WLON + WLON - LON_SHIFT:(p + 1) * WLON, :] = edge[:LON_SHIFT]

    t_val = table[...]
    t_hi = t_val.astype(BF16)
    t_rest = t_val - t_hi.astype(F32)
    t_mid = t_rest.astype(BF16)
    t_lo = (t_rest - t_mid.astype(F32)).astype(BF16)
    last_band = lax.axis_index("lat") == lax.axis_size("lat") - 1
    for lon_i in range(WLON):
        sel = selection(lon_i)
        b = mm(t_hi, sel) + mm(t_mid, sel) + mm(t_lo, sel)
        bias[:, lon_i, :] = b

    wq_all = w_qkv[...]
    for w in range(wins):
        xv = x[w]
        mean = jnp.mean(xv, axis=-1, keepdims=True)
        cen = xv - mean
        var = jnp.mean(cen * cen, axis=-1, keepdims=True)
        rs = lax.rsqrt(var + epsilon)
        xh = cen * rs
        xhat[w] = xh
        rstd_s[w] = rs
        nb = (xh * gain[...]).astype(BF16)
        normed[w] = nb
        res = mm(nb, wq_all).astype(BF16)
        for s in range(3):
            qkv[s, w] = res[:, s * width:(s + 1) * width]
        d_mix[w] = mm_nt(y[w].astype(BF16), w_proj[...]).astype(BF16)

    acc_o[...] = jnp.zeros_like(acc_o)
    acc_dq[...] = jnp.zeros_like(acc_dq)
    acc_dk[...] = jnp.zeros_like(acc_dk)
    acc_dv[...] = jnp.zeros_like(acc_dv)

    ri = lax.broadcasted_iota(jnp.int32, (WIN, WIN), 0)
    ci = lax.broadcasted_iota(jnp.int32, (WIN, WIN), 1)
    half = WIN // WLEV
    quarter = LAT_SHIFT * WLON

    def lev_of(n):
        return n >= half

    def lat_of(n):
        return jnp.where(n >= half, n - half, n) >= quarter

    lev_same = jnp.where(lev_of(ri) == lev_of(ci), 1, 0)
    lat_same = jnp.where(lat_of(ri) == lat_of(ci), 1, 0)
    lane = lax.broadcasted_iota(jnp.int32, (WIN, width), 1)

    def head_step(ah, carry):
        a = ah // HEADS
        h = ah - a * HEADS
        keep_lev = jnp.where(a == lev_wins - 1, 0, 1)
        keep_lat = jnp.where(last_band, 0, 1)
        same = ((lev_same + keep_lev) * (lat_same + keep_lat)) > 0
        bias_h = bias[pl.ds(ah * PLACES, PLACES)].reshape(WIN, WIN)
        bias_h = jnp.where(same, bias_h, masked_score)
        head = (lane >= h * head_width) & (lane < (h + 1) * head_width)
        d_bias_h = None
        for c in range(lon_wins):
            w = a * lon_wins + c
            q, k, v, dm = qkv[0, w], qkv[1, w], qkv[2, w], d_mix[w]
            zero = jnp.zeros_like(q)
            qm, km = jnp.where(head, q, zero), jnp.where(head, k, zero)
            vm, dmm = jnp.where(head, v, zero), jnp.where(head, dm, zero)
            s = mm_nt(q, km) * scale + bias_h
            m = jnp.max(s, axis=-1, keepdims=True)
            e = jnp.exp(s - m)
            pf = e / jnp.sum(e, axis=-1, keepdims=True)
            pb = pf.astype(BF16)
            acc_o[w] += mm(pb, vm)
            dp = mm_nt(dm, vm).astype(BF16).astype(F32)
            acc_dv[w] += mm_tn(pb, dmm)
            ds = pf * (dp - jnp.sum(dp * pf, axis=-1, keepdims=True))
            d_bias_h = ds if d_bias_h is None else d_bias_h + ds
            dsb = (ds * scale).astype(BF16)
            acc_dq[w] += mm(dsb, km)
            acc_dk[w] += mm_tn(dsb, qm)
        d_bias[pl.ds(ah * PLACES, PLACES)] = d_bias_h.reshape(PLACES, WLON, WIN)
        return carry

    lax.fori_loop(0, lev_wins * HEADS, head_step, 0)

    total = None
    for lon_i in range(WLON):
        part = mm_nt(d_bias[:, lon_i, :].astype(BF16), selection(lon_i))
        total = part if total is None else total + part
    d_table[...] = total.astype(d_table.dtype)

    stage[...] = jnp.zeros_like(stage)
    d_gain = jnp.zeros((1, width), F32)
    for w in range(wins):
        a, c = divmod(w, lon_wins)
        mb = acc_o[w].astype(BF16)
        mix[w] = mb
        for s, acc in enumerate((acc_dq, acc_dk, acc_dv)):
            dqkv[w, :, s * width:(s + 1) * width] = acc[w].astype(BF16)
        branch = mm(mb, w_proj[...])
        d_pre = mm_nt(dqkv[w], wq_all)
        xh = xhat[w]
        d_gain = d_gain + jnp.sum(d_pre * xh, axis=0, keepdims=True)
        g = d_pre * gain[...]
        dx = rstd_s[w] * (
            g - jnp.mean(g, axis=-1, keepdims=True) - xh * jnp.mean(g * xh, axis=-1, keepdims=True)
        )
        for n, val in enumerate((branch, dx)):
            for p in range(PLACES):
                l, t = divmod(p, WLAT)
                ol = (a * WLEV + l + WLEV // 2) % lev
                lo = LON_SHIFT + c * WLON
                stage[n, ol, t, lo:lo + WLON, :] = val[p * WLON:(p + 1) * WLON]
    out24[...] = stage[:, :, :, 0:cols, :].astype(BF16)
    out8[...] = stage[:, :, :, cols:cols + EDGE, :].astype(BF16)

    dwq = None
    dwp = None
    for w in range(wins):
        one = mm_tn(normed[w], dqkv[w])
        two = mm_tn(mix[w], y[w].astype(BF16))
        dwq = one if dwq is None else dwq + one
        dwp = two if dwp is None else dwp + two
    parts, share, _ = grads.shape
    per = width // parts
    for n in range(parts):
        grads[n, 0:per, 0:3 * width] = dwq[n * per:(n + 1) * per].astype(BF16)
        grads[n, 0:per, 3 * width:4 * width] = dwp[n * per:(n + 1) * per].astype(BF16)
        grads[n, per:share, 0:width] = jnp.broadcast_to(d_gain, (share - per, width)).astype(BF16)
        grads[n, per:share, width:4 * width] = jnp.zeros((share - per, 3 * width), BF16)


def core_call(air, up, east, north, corner, gain, w_qkv, w_proj, table, parts):
    lev, rows, cols, width = air.shape
    wins = (lev // WLEV) * (cols // WLON)
    pairs = (lev // WLEV) * HEADS
    share = width // parts + 8
    vm = lambda shape, dtype: pltpu.VMEM(shape, dtype)
    win_f = vm((wins, WIN, width), F32)
    win_b = vm((wins, WIN, width), BF16)
    spec = pl.BlockSpec(memory_space=pltpu.VMEM)
    return pl.pallas_call(
        core_kernel,
        out_shape=(
            jax.ShapeDtypeStruct((2, lev, rows, cols, width), BF16),
            jax.ShapeDtypeStruct((2, lev, rows, EDGE, width), BF16),
            jax.ShapeDtypeStruct((parts, share, 4 * width), BF16),
            jax.ShapeDtypeStruct(table.shape, BF16),
        ),
        in_specs=[spec] * 9,
        out_specs=(spec,) * 4,
        scratch_shapes=[
            win_f, win_f, win_f,
            vm((wins, WIN, 1), F32),
            win_b,
            vm((3, wins, WIN, width), BF16),
            win_b,
            vm((pairs * PLACES, WLON, WIN), F32),
            vm((pairs * PLACES, WLON, WIN), F32),
            win_f, win_f, win_f, win_f,
            vm((wins, WIN, 3 * width), BF16),
            win_b,
            vm((2, lev, rows, cols + EDGE, width), F32),
        ],
        compiler_params=pltpu.CompilerParams(vmem_limit_bytes=60 * 1024 * 1024),
        name="window_core",
    )(air, up, east, north, corner, gain, w_qkv, w_proj, table)


def from_behind(array, axis, by):
    peers = lax.axis_size(axis)
    return lax.ppermute(array, axis, [(i, (i + by) % peers) for i in range(peers)])


def on_device(air_state, upstream, norm_gain, w_qkv, w_proj, bias_table):
    lev, rows, cols, width = air_state.shape
    parts = lax.axis_size("lon")
    both = jnp.stack([air_state, upstream])
    east = from_behind(both[:, :, :, :EDGE], "lon", -1)
    north = from_behind(both[:, :, :LAT_SHIFT], "lat", -1)
    corner = from_behind(east[:, :, :LAT_SHIFT], "lat", -1)
    pairs = (lev // WLEV) * HEADS
    out24, out8, grads, d_table = core_call(
        air_state, upstream, east, north, corner, norm_gain.reshape(1, width), w_qkv, w_proj,
        bias_table.reshape(pairs * PLACES, PLACES * OFFS), parts,
    )
    keep = WLAT - LAT_SHIFT
    edge_west = from_behind(out8, "lon", 1)
    south24 = from_behind(out24[:, :, keep:], "lat", 1)
    south8 = from_behind(edge_west[:, :, keep:], "lat", 1)
    wide = jnp.concatenate([south24, out24[:, :, :keep]], axis=2)
    edge = jnp.concatenate([south8, edge_west[:, :, :keep]], axis=2)
    edge = jnp.pad(edge, ((0, 0), (0, 0), (0, 0), (0, cols - EDGE), (0, 0)))
    total = both.astype(F32) + wide.astype(F32) + edge.astype(F32)
    total = total.astype(BF16)
    grads = lax.psum(grads, ("lon", "lat")).astype(F32)
    d_table = lax.psum(d_table, "lon").astype(F32)
    per = width // parts
    d_wqkv = grads[:, :per, :3 * width].reshape(width, 3 * width)
    d_wproj = grads[:, :per, 3 * width:].reshape(width, width)
    d_gain = grads[0, per, :width]
    return total[0], total[1], d_gain, d_wqkv, d_wproj, d_table.reshape(bias_table.shape)


def solution(mesh):
    return jax.shard_map(
        on_device,
        mesh=mesh,
        in_specs=(
            P(None, "lat", "lon", None),
            P(None, "lat", "lon", None),
            P(),
            P(),
            P(),
            P("lat", None, None, None),
        ),
        out_specs=(
            P(None, "lat", "lon", None),
            P(None, "lat", "lon", None),
            P(),
            P(),
            P(),
            P("lat", None, None, None),
        ),
        check_vma=False,
    )
```

time: 288 us -> 250 us (0.87)
  waiting for transfers between devices: 94.2 us -> 189 us
  local copies, waits for them, and re-layouts: 91.5 us -> 10.1 us
  matrix products: 37.4 us -> 0 us
  Pallas kernels: 0 us -> 24 us
  blocking collectives: 24 us -> 0 us
  other arithmetic: 16.1 us -> 1.3 us
    psum x2, waiting for transfers between devices: 89.2 us -> 183 us  [the longest x1 134 us: on_device(): grads = lax.psum(grads, ('lon', 'lat')).astype(F32)]
    dot_general x13 -> x0, matrix products: 32.7 us -> none  [the longest x2 19.6 us: attention_core(): jnp.einsum('ahpqr,ijr->ahpiqj', picked, onehot, precision=lax.Precision.H...]
    add x3 -> x0, local copies, waits for them, and re-layouts: 31.6 us -> none  [the longest x2 31.5 us: attention_core(): scores = scores + expanded]
    pallas_call x0 -> x1, Pallas kernels: none -> 24 us  [core_call(): pl.pallas_call(core_kernel, out_shape=(jax.ShapeDtypeStruct((2, lev, rows...]
    psum x2 -> x0, blocking collectives: 24 us -> none  [the longest x1 12.2 us: on_device(): lax.psum(d_gain.astype(jnp.bfloat16), 'lat').astype(jnp.float32)]
    reshape x7 -> x2, local copies, waits for them, and re-layouts: 21.9 us -> 2.6 us  [the longest x1 1.75 us: on_device(): d_table.reshape(bias_table.shape)]
    convert_element_type x9 -> x1, other arithmetic: 7.83 us -> 0.22 us  [on_device(): total = total.astype(BF16)]
    squeeze x3 -> x1, local copies, waits for them, and re-layouts: 7.7 us -> 0.85 us  [on_device(): total[1]]
  transfers between devices with their start and end apart: 10 -> 8, of which waited for: 4 -> 4; matrix products, arithmetic and copies ran while one was open for 25% -> 3% of each run, Pallas kernels for 0% -> 0%
where the time goes in v1:
time: 250 us
  waiting for transfers between devices  189 us (76%)
  Pallas kernels  24 us (10%)
  between operations  14.1 us (6%)
  starting transfers between devices  11.3 us (5%)
  local copies, waits for them, and re-layouts  10.1 us (4%)
    psum x1, waiting for transfers between devices, on_device(): grads = lax.psum(grads, ('lon', 'lat')).astype(F32)  134 us
    psum x1, waiting for transfers between devices, on_device(): d_table = lax.psum(d_table, 'lon').astype(F32)  49.4 us
    pallas_call x1, Pallas kernels, core_call(): pl.pallas_call(core_kernel, out_shape=(jax.ShapeDtypeStruct((2, lev, rows...  24 us
    ppermute x6, starting transfers between devices, from_behind(): lax.ppermute(array, axis, [(i, (i + by) % peers) for i in range(peers)])  11.2 us
    ppermute x6, waiting for transfers between devices, from_behind(): lax.ppermute(array, axis, [(i, (i + by) % peers) for i in range(peers)])  5.89 us
  transfers between devices with their start and end apart: 8, of which 4 were waited for; matrix products, arithmetic and copies ran while one was open for 3% of the time, Pallas kernels for 0%

profile of v1, /device:TPU:0, one launch (start us, length us, event | category | flops | bytes accessed | tf_op | source)
XLA Modules:
  0.0 250.0 jit_solution(10099665226571955273)
XLA Ops:
  7.2 0.0 copy-start.2
  7.2 0.0 copy-start
  7.2 0.0 all-reduce.6.cloned.1.call-start
  7.2 1.0 fusion.4
  8.3 0.0 copy-start.7
  8.3 3.4 %collective-permute-start = (bf16[2,4,6,8,192]{4,3,2,1,0:T(8,128)(2,1)S(1)}, bf16[2,4,6,8,192]{4,3,2,1,0:T(8,128)(2,1)S(1)}, u32[]{:S(2)}, u32[]{:S(2)}) collective-permute-start(bf16[2,4,6,8,192]{4,3,2,1,0:T(8,128)(2,1)S(1)} %fusion.4), channel_id=1, source_target_pairs={{0,28},{4,0},{8,4},{12,8},{16,12},{20,16},{24,20},{28,24},{1,29},{... | collective-permute-start | bytes 442376 | tf_op jit(solution)/shard_map/ppermute | solution.py:251
  11.7 0.1 fusion.3
  11.8 3.7 %collective-permute-start.1 = (bf16[2,4,3,24,192]{4,3,2,1,0:T(8,128)(2,1)S(1)}, bf16[2,4,3,24,192]{4,3,2,1,0:T(8,128)(2,1)S(1)}, u32[]{:S(2)}, u32[]{:S(2)}) collective-permute-start(bf16[2,4,3,24,192]{4,3,2,1,0:T(8,128)(2,1)S(1)} %fusion.3), channel_id=1, source_target_pairs={{0,3},{1,0},{2,1},{3,2},{4,7},{5,4},{6,5},{7,6},{8,11},{9,8},{10,9... | collective-permute-start | bytes 663560 | tf_op jit(solution)/shard_map/ppermute | solution.py:251
  15.4 3.1 %collective-permute-start.2 = (bf16[2,4,3,8,192]{4,3,2,1,0:T(8,128)(2,1)S(1)}, bf16[2,4,3,8,192]{4,3,2,1,0:T(8,128)(2,1)S(1)}, u32[]{:S(2)}, u32[]{:S(2)}) collective-permute-start(bf16[2,4,3,8,192]{4,3,2,1,0:T(8,128)(2,1)S(1)} %slice.52), channel_id=1, source_target_pairs={{0,3},{1,0},{2,1},{3,2},{4,7},{5,4},{6,5},{7,6},{8,11},{9,8},{10,9... | collective-permute-start | bytes 221192 | tf_op jit(solution)/shard_map/ppermute | solution.py:251
  18.6 0.8 reshape.31.table
  19.4 3.1 %collective-permute-done.2.corner = bf16[2,4,3,8,192]{4,3,2,1,0:T(8,128)(2,1)S(1)} collective-permute-done((bf16[2,4,3,8,192]{4,3,2,1,0:T(8,128)(2,1)S(1)}, bf16[2,4,3,8,192]{4,3,2,1,0:T(8,128)(2,1)S(1)}, u32[]{:S(2)}, u32[]{:S(2)}) %collective-permute-start.2) | collective-permute-done | bytes 73760 | tf_op jit(solution)/shard_map/ppermute | solution.py:251
  22.6 0.0 collective-permute-done.1.north
  22.6 0.6 copy-done.8
  23.2 0.1 copy-done.6
  23.3 24.0 %window_core.1 = (bf16[2,4,6,24,192]{4,3,2,1,0:T(8,128)(2,1)}, bf16[2,4,6,8,192]{4,3,2,1,0:T(8,128)(2,1)}, bf16[8,32,768]{2,1,0:T(8,128)(2,1)}, bf16[144,276]{1,0:T(8,128)(2,1)}) custom-call(bf16[4,6,24,192]{3,2,1,0:T(8,128)(2,1)} %air.1, bf16[4,6,24,192]{3,2,1,0:T(8,128)(2,1)} %up.1, bf16[2,4,6,8,192]{4,3,2,1,0:T(8,128)(2,1)} %copy-done.5, ...), custom_call_target="tpu_custom_call" | custom-call | tf_op jit(solution)/shard_map/window_core/pallas_call | solution.py:221
  47.4 0.0 collective-permute-start.4
  47.4 1.8 reshape.34
  49.1 0.0 all-reduce.6.cloned.1.call-update
  49.1 0.0 all-reduce.4.cloned.1.call-start
  49.2 1.1 fusion.5
  50.3 0.5 collective-permute-start.3
  50.8 0.0 all-reduce.4.cloned.1.call-update
  50.8 2.7 %collective-permute-done.4 = bf16[2,4,6,8,192]{4,3,2,1,0:T(8,128)(2,1)S(1)} collective-permute-done((bf16[2,4,6,8,192]{4,3,2,1,0:T(8,128)(2,1)}, bf16[2,4,6,8,192]{4,3,2,1,0:T(8,128)(2,1)S(1)}, u32[]{:S(2)}, u32[]{:S(2)}) %collective-permute-start.4) | collective-permute-done | bytes 147488 | tf_op jit(solution)/shard_map/ppermute | solution.py:251
  53.6 0.5 collective-permute-start.5
  54.1 49.4 %all-reduce.6.cloned.1.call-done = bf16[1,2,6,3312]{3,2,1,0:T(8,128)(2,1)} async-done(((bf16[1,2,6,3312]{3,2,1,0:T(8,128)(2,1)}), bf16[1,2,6,3312]{3,2,1,0:T(8,128)(2,1)}) %all-reduce.6.cloned.1.call-update) | async-done | bytes 79504 | tf_op jit(solution)/shard_map/psum | solution.py:276
  103.5 1.6 copy.15
  105.2 133.7 %all-reduce.4.cloned.1.call-done = bf16[8,32,768]{2,1,0:T(8,128)(2,1)} async-done(((bf16[8,32,768]{2,1,0:T(8,128)(2,1)}), bf16[8,32,768]{2,1,0:T(8,128)(2,1)}) %all-reduce.4.cloned.1.call-update) | async-done | bytes 393232 | tf_op jit(solution)/shard_map/psum | solution.py:275
  238.9 1.8 slice.58
  240.7 0.8 slice.59
  241.5 0.6 slice.57
  242.1 0.2 add_convert_fusion
  242.3 0.8 slice_bitcast_fusion
  (19 shorter events, 0.1 us)
Async XLA Ops:
  7.2 4.5 %copy-start.2 = (bf16[4,6,24,192]{3,2,1,0:T(8,128)(2,1)S(1)}, bf16[4,6,24,192]{3,2,1,0:T(8,128)(2,1)}, u32[]{:S(2)}) copy-start(bf16[4,6,24,192]{3,2,1,0:T(8,128)(2,1)} %air.1) | copy-start | bytes 663556
  7.2 4.5 %copy-start = (bf16[4,6,24,192]{3,2,1,0:T(8,128)(2,1)S(1)}, bf16[4,6,24,192]{3,2,1,0:T(8,128)(2,1)}, u32[]{:S(2)}) copy-start(bf16[4,6,24,192]{3,2,1,0:T(8,128)(2,1)} %up.1) | copy-start | bytes 663556
  7.2 96.4 %all-reduce.6.cloned.1.call-start = ((), (), s32[]{:S(2)}) async-start(), calls=%async_computation.1 | async-start | bytes 212992 | tf_op jit(solution)/shard_map/psum | solution.py:276
  8.3 10.3 %copy-start.7 = (f32[1,2,6,3312]{3,1,2,0:T(2,128)S(1)}, f32[1,2,6,3312]{3,1,2,0:T(2,128)}, u32[]{:S(2)}) copy-start(f32[1,2,6,3312]{3,1,2,0:T(2,128)} %param.11) | copy-start | bytes 476932
  8.3 7.1 %collective-permute-start = (bf16[2,4,6,8,192]{4,3,2,1,0:T(8,128)(2,1)S(1)}, bf16[2,4,6,8,192]{4,3,2,1,0:T(8,128)(2,1)S(1)}, u32[]{:S(2)}, u32[]{:S(2)}) collective-permute-start(bf16[2,4,6,8,192]{4,3,2,1,0:T(8,128)(2,1)S(1)} %fusion.4), channel_id=1, source_target_pairs={{0,28},{4,0},{8,4},{12,8},{16,12},{20,16},{24,20},{28,24},{1,29},{... | collective-permute-start | bytes 442376 | tf_op jit(solution)/shard_map/ppermute | solution.py:251
  11.8 10.8 %collective-permute-start.1 = (bf16[2,4,3,24,192]{4,3,2,1,0:T(8,128)(2,1)S(1)}, bf16[2,4,3,24,192]{4,3,2,1,0:T(8,128)(2,1)S(1)}, u32[]{:S(2)}, u32[]{:S(2)}) collective-permute-start(bf16[2,4,3,24,192]{4,3,2,1,0:T(8,128)(2,1)S(1)} %fusion.3), channel_id=1, source_target_pairs={{0,3},{1,0},{2,1},{3,2},{4,7},{5,4},{6,5},{7,6},{8,11},{9,8},{10,9... | collective-permute-start | bytes 663560 | tf_op jit(solution)/shard_map/ppermute | solution.py:251
  15.4 7.2 %copy-start.5 = (bf16[2,4,6,8,192]{4,3,2,1,0:T(8,128)(2,1)}, bf16[2,4,6,8,192]{4,3,2,1,0:T(8,128)(2,1)S(1)}, u32[]{:S(2)}) copy-start(bf16[2,4,6,8,192]{4,3,2,1,0:T(8,128)(2,1)S(1)} %collective-permute-done.east) | copy-start | bytes 442372
  15.4 7.1 %collective-permute-start.2 = (bf16[2,4,3,8,192]{4,3,2,1,0:T(8,128)(2,1)S(1)}, bf16[2,4,3,8,192]{4,3,2,1,0:T(8,128)(2,1)S(1)}, u32[]{:S(2)}, u32[]{:S(2)}) collective-permute-start(bf16[2,4,3,8,192]{4,3,2,1,0:T(8,128)(2,1)S(1)} %slice.52), channel_id=1, source_target_pairs={{0,3},{1,0},{2,1},{3,2},{4,7},{5,4},{6,5},{7,6},{8,11},{9,8},{10,9... | collective-permute-start | bytes 221192 | tf_op jit(solution)/shard_map/ppermute | solution.py:251
  22.6 0.6 copy-start.8
  22.6 0.7 copy-start.6
  47.4 6.2 %collective-permute-start.4 = (bf16[2,4,6,8,192]{4,3,2,1,0:T(8,128)(2,1)}, bf16[2,4,6,8,192]{4,3,2,1,0:T(8,128)(2,1)S(1)}, u32[]{:S(2)}, u32[]{:S(2)}) collective-permute-start(bf16[2,4,6,8,192]{4,3,2,1,0:T(8,128)(2,1)} %get-tuple-element.11), channel_id=1, source_target_pairs={{0,4},{4,8},{8,12},{12,16},{16,20},{20,24},{24,28},{28,0},{1,5},{5... | collective-permute-start | bytes 442376 | tf_op jit(solution)/shard_map/ppermute | solution.py:251
  49.1 189.8 %all-reduce.4.cloned.1.call-start = ((), (), s32[]{:S(2)}) async-start(), calls=%async_computation | async-start | bytes 786432 | tf_op jit(solution)/shard_map/psum | solution.py:275
  50.3 191.8 %collective-permute-start.3 = (bf16[2,4,3,24,192]{4,3,2,1,0:T(8,128)(2,1)S(1)}, bf16[2,4,3,24,192]{4,3,2,1,0:T(8,128)(2,1)S(1)}, u32[]{:S(2)}, u32[]{:S(2)}) collective-permute-start(bf16[2,4,3,24,192]{4,3,2,1,0:T(8,128)(2,1)S(1)} %get-tuple-element.22), channel_id=1, source_target_pairs={{0,1},{1,2},{2,3},{3,0},{4,5},{5,6},{6,7},{7,4},{8,9},{9,10},{10,1... | collective-permute-start | bytes 663560 | tf_op jit(solution)/shard_map/ppermute | solution.py:251
  53.6 188.5 %collective-permute-start.5 = (bf16[2,4,3,8,192]{4,3,2,1,0:T(8,128)(2,1)S(1)}, bf16[2,4,3,8,192]{4,3,2,1,0:T(8,128)(2,1)S(1)}, u32[]{:S(2)}, u32[]{:S(2)}) collective-permute-start(bf16[2,4,3,8,192]{4,3,2,1,0:T(8,128)(2,1)S(1)} %get-tuple-element.24), channel_id=1, source_target_pairs={{0,1},{1,2},{2,3},{3,0},{4,5},{5,6},{6,7},{7,4},{8,9},{9,10},{10,1... | collective-permute-start | bytes 221192 | tf_op jit(solution)/shard_map/ppermute | solution.py:251
  105.2 136.9 %copy-start.1 = (bf16[4,6,24,192]{3,2,1,0:T(8,128)(2,1)S(1)}, bf16[4,6,24,192]{3,2,1,0:T(8,128)(2,1)}, u32[]{:S(2)}) copy-start(bf16[4,6,24,192]{3,2,1,0:T(8,128)(2,1)} %up.1) | copy-start | bytes 663556
  105.2 136.9 %copy-start.3 = (bf16[4,6,24,192]{3,2,1,0:T(8,128)(2,1)S(1)}, bf16[4,6,24,192]{3,2,1,0:T(8,128)(2,1)}, u32[]{:S(2)}) copy-start(bf16[4,6,24,192]{3,2,1,0:T(8,128)(2,1)} %air.1) | copy-start | bytes 663556
  238.9 1.8 copy-start.4
Sparse Core Ops, SparseCore 0:
  49.3 54.2 all-reduce.5
  109.4 129.4 all-reduce.3

commit v2 on v1

--- a/solution.py
+++ b/solution.py
@@ -166,7 +166,9 @@
     for lon_i in range(WLON):
         part = mm_nt(d_bias[:, lon_i, :].astype(BF16), selection(lon_i))
         total = part if total is None else total + part
-    d_table[...] = total.astype(d_table.dtype)
+    t_parts, t_per, _ = d_table.shape
+    for n in range(t_parts):
+        d_table[n] = total[n * t_per:(n + 1) * t_per].astype(BF16)
 
     stage[...] = jnp.zeros_like(stage)
     d_gain = jnp.zeros((1, width), F32)
@@ -224,7 +226,7 @@
             jax.ShapeDtypeStruct((2, lev, rows, cols, width), BF16),
             jax.ShapeDtypeStruct((2, lev, rows, EDGE, width), BF16),
             jax.ShapeDtypeStruct((parts, share, 4 * width), BF16),
-            jax.ShapeDtypeStruct(table.shape, BF16),
+            jax.ShapeDtypeStruct((parts, table.shape[0] // parts, table.shape[1]), BF16),
         ),
         in_specs=[spec] * 9,
         out_specs=(spec,) * 4,
@@ -246,39 +248,213 @@
     )(air, up, east, north, corner, gain, w_qkv, w_proj, table)
 
 
-def from_behind(array, axis, by):
-    peers = lax.axis_size(axis)
-    return lax.ppermute(array, axis, [(i, (i + by) % peers) for i in range(peers)])
+def spot(lon=0, lat=0):
+    lon_at = lax.rem(lax.axis_index("lon") + lon + lax.axis_size("lon"), lax.axis_size("lon"))
+    lat_at = lax.rem(lax.axis_index("lat") + lat + lax.axis_size("lat"), lax.axis_size("lat"))
+    return {"lon": lon_at, "lat": lat_at}
+
+
+def greet(places):
+    barrier = pltpu.get_barrier_semaphore()
+    for place in places:
+        pl.semaphore_signal(barrier, inc=1, device_id=place, device_id_type=pl.DeviceIdType.MESH)
+    pl.semaphore_wait(barrier, len(places))
+
+
+def remote(src, dst, send, recv, place):
+    return pltpu.make_async_remote_copy(
+        src_ref=src, dst_ref=dst, send_sem=send, recv_sem=recv,
+        device_id=place, device_id_type=pl.DeviceIdType.MESH,
+    )
+
+
+def halo_kernel(air, up, east, north, corner, send, recv):
+    greet([spot(-1, 0), spot(0, -1), spot(-1, -1), spot(1, 0), spot(0, 1), spot(1, 1)])
+    copies = []
+    for n, src in enumerate((air, up)):
+        rim = pl.ds(0, LAT_SHIFT)
+        edge = pl.ds(0, EDGE)
+        copies += [
+            remote(src.at[:, rim], north.at[n], send.at[n, 0], recv.at[n, 0], spot(0, -1)),
+            remote(src.at[:, :, edge], east.at[n], send.at[n, 1], recv.at[n, 1], spot(-1, 0)),
+            remote(src.at[:, rim, edge], corner.at[n], send.at[n, 2], recv.at[n, 2], spot(-1, -1)),
+        ]
+    for copy in copies:
+        copy.start()
+    for copy in copies:
+        copy.wait()
+
+
+def halo_call(air, up):
+    lev, rows, cols, width = air.shape
+    spec = pl.BlockSpec(memory_space=pltpu.VMEM)
+    return pl.pallas_call(
+        halo_kernel,
+        out_shape=(
+            jax.ShapeDtypeStruct((2, lev, rows, EDGE, width), BF16),
+            jax.ShapeDtypeStruct((2, lev, LAT_SHIFT, cols, width), BF16),
+            jax.ShapeDtypeStruct((2, lev, LAT_SHIFT, EDGE, width), BF16),
+        ),
+        in_specs=[spec] * 2,
+        out_specs=(spec,) * 3,
+        scratch_shapes=[pltpu.SemaphoreType.DMA((2, 3)), pltpu.SemaphoreType.DMA((2, 3))],
+        compiler_params=pltpu.CompilerParams(
+            collective_id=0, has_side_effects=True, vmem_limit_bytes=40 * 1024 * 1024
+        ),
+        name="halo_in",
+    )(air, up)
+
+
+def finish_kernel(
+    lons, lats, air, up, out24, out8, grads, table,
+    block_out, d_state, d_gain, d_wqkv, d_wproj, d_table,
+    got_n, got_e, got_c, land_w, land_t, land_lat, all_w, all_t,
+    h_send, h_recv, w_send, w_recv, t_send, t_recv, l_send, l_recv, gw_send, gw_recv, gt_send, gt_recv,
+):
+    me, me_lat = lax.axis_index("lon"), lax.axis_index("lat")
+    rows, width = air.shape[1], air.shape[3]
+    keep = rows - LAT_SHIFT
+    greet(
+        [spot(k, 0) for k in range(1, lons)]
+        + [spot(0, k) for k in range(1, lats)]
+        + [spot(1, 1), spot(-1, -1)]
+    )
+    w_copies, t_copies = [], []
+    for k in range(1, lons):
+        to = spot(k, 0)
+        w_copies.append(remote(grads.at[to["lon"]], land_w.at[k - 1], w_send.at[k - 1], w_recv.at[k - 1], to))
+        t_copies.append(remote(table.at[to["lon"]], land_t.at[k - 1], t_send.at[k - 1], t_recv.at[k - 1], to))
+    rim = pl.ds(keep, LAT_SHIFT)
+    own = pl.ds(0, keep)
+    halos = [
+        remote(out24.at[:, :, rim], got_n, h_send.at[0], h_recv.at[0], spot(0, 1)),
+        remote(out8.at[:, :, own], got_e, h_send.at[1], h_recv.at[1], spot(1, 0)),
+        remote(out8.at[:, :, rim], got_c, h_send.at[2], h_recv.at[2], spot(1, 1)),
+    ]
+    for copy in w_copies + halos + t_copies:
+        copy.start()
+
+    total = grads[me].astype(F32)
+    for k in range(1, lons):
+        w_copies[k - 1].wait_recv()
+        total = total + land_w[k - 1].astype(F32)
+    land_lat[me_lat] = total.astype(BF16)
+    l_copies = [
+        remote(land_lat.at[me_lat], land_lat.at[me_lat], l_send.at[k - 1], l_recv.at[k - 1], spot(0, k))
+        for k in range(1, lats)
+    ]
+    for copy in l_copies:
+        copy.start()
+
+    total = table[me].astype(F32)
+    for k in range(1, lons):
+        t_copies[k - 1].wait_recv()
+        total = total + land_t[k - 1].astype(F32)
+    all_t[me] = total.astype(BF16)
+    gt_copies = [
+        remote(all_t.at[me], all_t.at[me], gt_send.at[k - 1], gt_recv.at[k - 1], spot(k, 0))
+        for k in range(1, lons)
+    ]
+    for copy in gt_copies:
+        copy.start()
+
+    for copy in halos:
+        copy.wait_recv()
+    for n, (src, dst) in enumerate(((air, block_out), (up, d_state))):
+        for lv in range(air.shape[0]):
+            for r in range(rows):
+                base = src[lv, r].astype(F32)
+                if r < LAT_SHIFT:
+                    wide, edge = got_n[n, lv, r], got_c[n, lv, r]
+                else:
+                    wide, edge = out24[n, lv, r - LAT_SHIFT], got_e[n, lv, r - LAT_SHIFT]
+                base = base + wide.astype(F32)
+                head = base[:EDGE] + edge.astype(F32)
+                dst[lv, r] = jnp.concatenate([head, base[EDGE:]], axis=0).astype(BF16)
+
+    for copy in l_copies:
+        copy.wait_recv()
+    total = land_lat[0].astype(F32)
+    for k in range(1, lats):
+        total = total + land_lat[k].astype(F32)
+    all_w[me] = total.astype(BF16)
+    gw_copies = [
+        remote(all_w.at[me], all_w.at[me], gw_send.at[k - 1], gw_recv.at[k - 1], spot(k, 0))
+        for k in range(1, lons)
+    ]
+    for copy in gw_copies:
+        copy.start()
+
+    for copy in gt_copies:
+        copy.wait_recv()
+    d_table[...] = all_t[...].astype(F32)
+    for copy in gw_copies:
+        copy.wait_recv()
+    per = width // lons
+    d_wqkv[...] = all_w[:, 0:per, 0:3 * width].astype(F32)
+    d_wproj[...] = all_w[:, 0:per, 3 * width:4 * width].astype(F32)
+    d_gain[...] = all_w[0, per:per + 8, 0:width].astype(F32)
+    for copy in w_copies + t_copies + halos + l_copies + gt_copies + gw_copies:
+        copy.wait_send()
+
+
+def finish_call(air, up, out24, out8, grads, table, lats):
+    lev, rows, cols, width = air.shape
+    lons, share, wide = grads.shape
+    spec = pl.BlockSpec(memory_space=pltpu.VMEM)
+    dma = pltpu.SemaphoreType.DMA
+    per = width // lons
+    return pl.pallas_call(
+        partial(finish_kernel, lons, lats),
+        out_shape=(
+            jax.ShapeDtypeStruct(air.shape, BF16),
+            jax.ShapeDtypeStruct(air.shape, BF16),
+            jax.ShapeDtypeStruct((8, width), F32),
+            jax.ShapeDtypeStruct((lons, per, 3 * width), F32),
+            jax.ShapeDtypeStruct((lons, per, width), F32),
+            jax.ShapeDtypeStruct(table.shape, F32),
+        ),
+        in_specs=[spec] * 6,
+        out_specs=(spec,) * 6,
+        scratch_shapes=[
+            pltpu.VMEM((2, lev, LAT_SHIFT, cols, width), BF16),
+            pltpu.VMEM((2, lev, rows - LAT_SHIFT, EDGE, width), BF16),
+            pltpu.VMEM((2, lev, LAT_SHIFT, EDGE, width), BF16),
+            pltpu.VMEM((lons - 1, share, wide), BF16),
+            pltpu.VMEM((lons - 1,) + table.shape[1:], BF16),
+            pltpu.VMEM((lats, share, wide), BF16),
+            pltpu.VMEM(grads.shape, BF16),
+            pltpu.VMEM(table.shape, BF16),
+            dma((3,)), dma((3,)),
+            dma((lons - 1,)), dma((lons - 1,)),
+            dma((lons - 1,)), dma((lons - 1,)),
+            dma((lats - 1,)), dma((lats - 1,)),
+            dma((lons - 1,)), dma((lons - 1,)),
+            dma((lons - 1,)), dma((lons - 1,)),
+        ],
+        compiler_params=pltpu.CompilerParams(
+            collective_id=1, has_side_effects=True, vmem_limit_bytes=40 * 1024 * 1024
+        ),
+        name="finish",
+    )(air, up, out24, out8, grads, table)
 
 
 def on_device(air_state, upstream, norm_gain, w_qkv, w_proj, bias_table):
     lev, rows, cols, width = air_state.shape
-    parts = lax.axis_size("lon")
-    both = jnp.stack([air_state, upstream])
-    east = from_behind(both[:, :, :, :EDGE], "lon", -1)
-    north = from_behind(both[:, :, :LAT_SHIFT], "lat", -1)
-    corner = from_behind(east[:, :, :LAT_SHIFT], "lat", -1)
+    lons, lats = lax.axis_size("lon"), lax.axis_size("lat")
     pairs = (lev // WLEV) * HEADS
+    east, north, corner = halo_call(air_state, upstream)
     out24, out8, grads, d_table = core_call(
         air_state, upstream, east, north, corner, norm_gain.reshape(1, width), w_qkv, w_proj,
-        bias_table.reshape(pairs * PLACES, PLACES * OFFS), parts,
-    )
-    keep = WLAT - LAT_SHIFT
-    edge_west = from_behind(out8, "lon", 1)
-    south24 = from_behind(out24[:, :, keep:], "lat", 1)
-    south8 = from_behind(edge_west[:, :, keep:], "lat", 1)
-    wide = jnp.concatenate([south24, out24[:, :, :keep]], axis=2)
-    edge = jnp.concatenate([south8, edge_west[:, :, :keep]], axis=2)
-    edge = jnp.pad(edge, ((0, 0), (0, 0), (0, 0), (0, cols - EDGE), (0, 0)))
-    total = both.astype(F32) + wide.astype(F32) + edge.astype(F32)
-    total = total.astype(BF16)
-    grads = lax.psum(grads, ("lon", "lat")).astype(F32)
-    d_table = lax.psum(d_table, "lon").astype(F32)
-    per = width // parts
-    d_wqkv = grads[:, :per, :3 * width].reshape(width, 3 * width)
-    d_wproj = grads[:, :per, 3 * width:].reshape(width, width)
-    d_gain = grads[0, per, :width]
-    return total[0], total[1], d_gain, d_wqkv, d_wproj, d_table.reshape(bias_table.shape)
+        bias_table.reshape(pairs * PLACES, PLACES * OFFS), lons,
+    )
+    block_out, d_state, d_gain, d_wqkv, d_wproj, d_table = finish_call(
+        air_state, upstream, out24, out8, grads, d_table, lats
+    )
+    return (
+        block_out, d_state, d_gain[0], d_wqkv.reshape(width, 3 * width), d_wproj.reshape(width, width),
+        d_table.reshape(bias_table.shape),
+    )
 
 
 def solution(mesh):

time: 250 us -> 77.2 us (0.31)
  waiting for transfers between devices: 189 us -> 0 us
  Pallas kernels: 24 us -> 64 us
  between operations: 14.1 us -> 0.7 us
  starting transfers between devices: 11.3 us -> 0 us
    psum x2 -> x0, waiting for transfers between devices: 183 us -> none  [the longest x1 134 us: on_device(): grads = lax.psum(grads, ('lon', 'lat')).astype(F32)]
    pallas_call x0 -> x2, Pallas kernels: none -> 39.8 us  [the longest x1 24.8 us: finish_call(): pl.pallas_call(partial(finish_kernel, lons, lats), out_shape=(jax.ShapeDt...]
    ppermute x6 -> x0, starting transfers between devices: 11.2 us -> none  [from_behind(): lax.ppermute(array, axis, [(i, (i + by) % peers) for i in range(peers)])]
    unnamed x20 -> x28, local copies, waits for them, and re-layouts: 2.42 us -> 10.6 us
    ppermute x6 -> x0, waiting for transfers between devices: 5.89 us -> none  [from_behind(): lax.ppermute(array, axis, [(i, (i + by) % peers) for i in range(peers)])]
    slice x6 -> x1, local copies, waits for them, and re-layouts: 4.28 us -> 0.56 us  [on_device(): d_gain[0]]
  transfers between devices with their start and end apart: 8 -> 0, of which waited for: 4 -> 0; matrix products, arithmetic and copies ran while one was open for 3% -> 0% of each run, Pallas kernels for 0% -> 0%
where the time goes in v2:
time: 77.2 us; the launch traced here: 76.9 us
  Pallas kernels  64 us (83%)
  local copies, waits for them, and re-layouts  12.2 us (16%)
    pallas_call x1, Pallas kernels, finish_call(): pl.pallas_call(partial(finish_kernel, lons, lats), out_shape=(jax.ShapeDt...  24.8 us
    pallas_call x1, Pallas kernels, core_call(): pl.pallas_call(core_kernel, out_shape=(jax.ShapeDtypeStruct((2, lev, rows...  24.1 us
    pallas_call x1, Pallas kernels, halo_call(): pl.pallas_call(halo_kernel, out_shape=(jax.ShapeDtypeStruct((2, lev, rows...  15 us
    unnamed x28, local copies, waits for them, and re-layouts  10.6 us

profile of v2, /device:TPU:0, one launch (start us, length us, event | category | flops | bytes accessed | tf_op | source)
XLA Modules:
  0.0 76.9 jit_solution(6787041003403352774)
XLA Ops:
  0.6 0.0 copy-start.2
  0.6 1.0 %copy.14 = f32[1,2,6,3312]{3,2,1,0:T(8,128)S(1)} copy(f32[1,2,6,3312]{3,1,2,0:T(2,128)} %param.11) | data formatting | bytes 317952 | tf_op args[5]
  1.6 0.0 copy-start
  1.6 0.8 %reshape.28.table = f32[144,276]{1,0:T(8,128)} reshape(f32[1,2,6,3312]{3,2,1,0:T(8,128)S(1)} %copy.14) | data formatting | bytes 317952 | tf_op jit(solution)/shard_map/reshape | solution.py:449
  2.5 0.0 copy-done.2
  2.5 0.1 copy-done
  2.6 15.0 %halo_in.1 = (bf16[2,4,6,8,192]{4,3,2,1,0:T(8,128)(2,1)S(1)}, bf16[2,4,3,24,192]{4,3,2,1,0:T(8,128)(2,1)S(1)}, bf16[2,4,3,8,192]{4,3,2,1,0:T(8,128)(2,1)S(1)}) custom-call(bf16[4,6,24,192]{3,2,1,0:T(8,128)(2,1)S(1)} %copy-done, bf16[4,6,24,192]{3,2,1,0:T(8,128)(2,1)S(1)} %copy-done.2), custom_call_target="tpu_custom_call" | custom-call | tf_op jit(solution)/shard_map/halo_in/pallas_call | solution.py:291
  17.6 0.0 copy-start.6
  17.6 0.7 copy-done.6
  18.3 0.0 copy-start.8
  18.3 0.7 copy-done.8
  19.0 0.0 copy-start.10
  19.0 0.6 copy-done.10
  19.6 0.0 copy-start.1
  19.7 0.0 copy-start.3
  19.7 24.1 %window_core.1 = (bf16[2,4,6,24,192]{4,3,2,1,0:T(8,128)(2,1)}, bf16[2,4,6,8,192]{4,3,2,1,0:T(8,128)(2,1)}, bf16[8,32,768]{2,1,0:T(8,128)(2,1)}, bf16[8,18,276]{2,1,0:T(8,128)(2,1)}) custom-call(bf16[4,6,24,192]{3,2,1,0:T(8,128)(2,1)} %air.5, bf16[4,6,24,192]{3,2,1,0:T(8,128)(2,1)} %up.5, bf16[2,4,6,8,192]{4,3,2,1,0:T(8,128)(2,1)} %copy-done.8, ...), custom_call_target="tpu_custom_call" | custom-call | tf_op jit(solution)/shard_map/window_core/pallas_call | solution.py:223
  43.8 0.0 copy-done.1
  43.8 0.0 copy-done.3
  43.8 0.0 copy-start.4
  43.8 1.1 %copy-done.4 = bf16[2,4,6,24,192]{4,3,2,1,0:T(8,128)(2,1)S(1)} copy-done((bf16[2,4,6,24,192]{4,3,2,1,0:T(8,128)(2,1)S(1)}, bf16[2,4,6,24,192]{4,3,2,1,0:T(8,128)(2,1)}, u32[]{:S(2)}) %copy-start.4) | copy-done | bytes 442392
  44.9 1.0 %copy-done.5 = bf16[8,32,768]{2,1,0:T(8,128)(2,1)S(1)} copy-done((bf16[8,32,768]{2,1,0:T(8,128)(2,1)S(1)}, bf16[8,32,768]{2,1,0:T(8,128)(2,1)}, u32[]{:S(2)}) %copy-start.5) | copy-done | bytes 393240
  45.9 0.0 copy-start.7
  45.9 0.9 %copy-done.7 = bf16[2,4,6,8,192]{4,3,2,1,0:T(8,128)(2,1)S(1)} copy-done((bf16[2,4,6,8,192]{4,3,2,1,0:T(8,128)(2,1)S(1)}, bf16[2,4,6,8,192]{4,3,2,1,0:T(8,128)(2,1)}, u32[]{:S(2)}) %copy-start.7) | copy-done | bytes 147480
  46.8 0.9 %copy-done.9 = bf16[8,18,276]{2,1,0:T(8,128)(2,1)S(1)} copy-done((bf16[8,18,276]{2,1,0:T(8,128)(2,1)S(1)}, bf16[8,18,276]{2,1,0:T(8,128)(2,1)}, u32[]{:S(2)}) %copy-start.9) | copy-done | bytes 79512
  47.7 24.8 %finish.1 = (bf16[4,6,24,192]{3,2,1,0:T(8,128)(2,1)S(1)}, bf16[4,6,24,192]{3,2,1,0:T(8,128)(2,1)S(1)}, f32[8,192]{1,0:T(8,128)S(1)}, f32[8,24,576]{2,1,0:T(8,128...) custom-call(bf16[4,6,24,192]{3,2,1,0:T(8,128)(2,1)S(1)} %copy-done.1, bf16[4,6,24,192]{3,2,1,0:T(8,128)(2,1)S(1)} %copy-done.3, ...), custom_call_target="tpu_custom_call" | custom-call | tf_op jit(solution)/shard_map/finish/pallas_call | solution.py:407
  72.5 0.6 slice.3
  73.1 0.2 reshape.31
  73.3 0.7 copy.15
  74.0 0.7 copy.20
  74.7 0.7 copy.21
  75.4 0.8 %copy.22 = f32[192,576]{1,0:T(8,128)} copy(f32[192,576]{1,0:T(8,128)S(1)} %bitcast.4) | data formatting | bytes 884736
  76.2 0.7 copy.23
  (2 shorter events, 0.0 us)
Async XLA Ops:
  0.6 1.9 %copy-start.2 = (bf16[4,6,24,192]{3,2,1,0:T(8,128)(2,1)S(1)}, bf16[4,6,24,192]{3,2,1,0:T(8,128)(2,1)}, u32[]{:S(2)}) copy-start(bf16[4,6,24,192]{3,2,1,0:T(8,128)(2,1)} %up.5) | copy-start | bytes 663556
  1.6 1.0 %copy-start = (bf16[4,6,24,192]{3,2,1,0:T(8,128)(2,1)S(1)}, bf16[4,6,24,192]{3,2,1,0:T(8,128)(2,1)}, u32[]{:S(2)}) copy-start(bf16[4,6,24,192]{3,2,1,0:T(8,128)(2,1)} %air.5) | copy-start | bytes 663556
  17.6 0.7 copy-start.6
  18.3 0.7 copy-start.8
  19.0 0.6 copy-start.10
  19.6 24.2 %copy-start.1 = (bf16[4,6,24,192]{3,2,1,0:T(8,128)(2,1)S(1)}, bf16[4,6,24,192]{3,2,1,0:T(8,128)(2,1)}, u32[]{:S(2)}) copy-start(bf16[4,6,24,192]{3,2,1,0:T(8,128)(2,1)} %air.5) | copy-start | bytes 663556
  19.7 24.2 %copy-start.3 = (bf16[4,6,24,192]{3,2,1,0:T(8,128)(2,1)S(1)}, bf16[4,6,24,192]{3,2,1,0:T(8,128)(2,1)}, u32[]{:S(2)}) copy-start(bf16[4,6,24,192]{3,2,1,0:T(8,128)(2,1)} %up.5) | copy-start | bytes 663556
  43.8 1.1 %copy-start.4 = (bf16[2,4,6,24,192]{4,3,2,1,0:T(8,128)(2,1)S(1)}, bf16[2,4,6,24,192]{4,3,2,1,0:T(8,128)(2,1)}, u32[]{:S(2)}) copy-start(bf16[2,4,6,24,192]{4,3,2,1,0:T(8,128)(2,1)} %get-tuple-element.22.out24) | copy-start | bytes 1327108
  44.9 1.0 %copy-start.5 = (bf16[8,32,768]{2,1,0:T(8,128)(2,1)S(1)}, bf16[8,32,768]{2,1,0:T(8,128)(2,1)}, u32[]{:S(2)}) copy-start(bf16[8,32,768]{2,1,0:T(8,128)(2,1)} %get-tuple-element.24.grads) | copy-start | bytes 1179652
  45.9 0.9 %copy-start.7 = (bf16[2,4,6,8,192]{4,3,2,1,0:T(8,128)(2,1)S(1)}, bf16[2,4,6,8,192]{4,3,2,1,0:T(8,128)(2,1)}, u32[]{:S(2)}) copy-start(bf16[2,4,6,8,192]{4,3,2,1,0:T(8,128)(2,1)} %get-tuple-element.23.out8) | copy-start | bytes 442372
  46.8 0.9 %copy-start.9 = (bf16[8,18,276]{2,1,0:T(8,128)(2,1)S(1)}, bf16[8,18,276]{2,1,0:T(8,128)(2,1)}, u32[]{:S(2)}) copy-start(bf16[8,18,276]{2,1,0:T(8,128)(2,1)} %get-tuple-element.25.table) | copy-start | bytes 238468

commit v3 on v2

--- a/solution.py
+++ b/solution.py
@@ -160,15 +160,13 @@
         d_bias[pl.ds(ah * PLACES, PLACES)] = d_bias_h.reshape(PLACES, WLON, WIN)
         return carry
 
-    lax.fori_loop(0, lev_wins * HEADS, head_step, 0)
+    lax.fori_loop(0, lev_wins * HEADS, head_step, 0, unroll=2)
 
     total = None
     for lon_i in range(WLON):
         part = mm_nt(d_bias[:, lon_i, :].astype(BF16), selection(lon_i))
         total = part if total is None else total + part
-    t_parts, t_per, _ = d_table.shape
-    for n in range(t_parts):
-        d_table[n] = total[n * t_per:(n + 1) * t_per].astype(BF16)
+    t_total = total
 
     stage[...] = jnp.zeros_like(stage)
     d_gain = jnp.zeros((1, width), F32)
@@ -202,20 +200,23 @@
         two = mm_tn(mix[w], y[w].astype(BF16))
         dwq = one if dwq is None else dwq + one
         dwp = two if dwp is None else dwp + two
-    parts, share, _ = grads.shape
-    per = width // parts
+    parts, per, _ = grads.shape
+    t_share = d_table.shape[1]
+    t_per = t_total.shape[0] // parts
+    filler = jnp.concatenate([d_gain, jnp.zeros((1, t_total.shape[1] - width), F32)], axis=1)
+    filler = jnp.broadcast_to(filler, (t_share - t_per, t_total.shape[1]))
     for n in range(parts):
-        grads[n, 0:per, 0:3 * width] = dwq[n * per:(n + 1) * per].astype(BF16)
-        grads[n, 0:per, 3 * width:4 * width] = dwp[n * per:(n + 1) * per].astype(BF16)
-        grads[n, per:share, 0:width] = jnp.broadcast_to(d_gain, (share - per, width)).astype(BF16)
-        grads[n, per:share, width:4 * width] = jnp.zeros((share - per, 3 * width), BF16)
+        grads[n, :, 0:3 * width] = dwq[n * per:(n + 1) * per].astype(BF16)
+        grads[n, :, 3 * width:4 * width] = dwp[n * per:(n + 1) * per].astype(BF16)
+        rows_n = jnp.concatenate([t_total[n * t_per:(n + 1) * t_per], filler], axis=0)
+        d_table[n] = rows_n.astype(BF16)
 
 
 def core_call(air, up, east, north, corner, gain, w_qkv, w_proj, table, parts):
     lev, rows, cols, width = air.shape
     wins = (lev // WLEV) * (cols // WLON)
     pairs = (lev // WLEV) * HEADS
-    share = width // parts + 8
+    t_share = table.shape[0] // parts // 8 * 8 + 8
     vm = lambda shape, dtype: pltpu.VMEM(shape, dtype)
     win_f = vm((wins, WIN, width), F32)
     win_b = vm((wins, WIN, width), BF16)
@@ -225,8 +226,8 @@
         out_shape=(
             jax.ShapeDtypeStruct((2, lev, rows, cols, width), BF16),
             jax.ShapeDtypeStruct((2, lev, rows, EDGE, width), BF16),
-            jax.ShapeDtypeStruct((parts, share, 4 * width), BF16),
-            jax.ShapeDtypeStruct((parts, table.shape[0] // parts, table.shape[1]), BF16),
+            jax.ShapeDtypeStruct((parts, width // parts, 4 * width), BF16),
+            jax.ShapeDtypeStruct((parts, t_share, table.shape[1]), BF16),
         ),
         in_specs=[spec] * 9,
         out_specs=(spec,) * 4,
@@ -243,7 +244,7 @@
             win_b,
             vm((2, lev, rows, cols + EDGE, width), F32),
         ],
-        compiler_params=pltpu.CompilerParams(vmem_limit_bytes=60 * 1024 * 1024),
+        compiler_params=pltpu.CompilerParams(vmem_limit_bytes=26 * 1024 * 1024),
         name="window_core",
     )(air, up, east, north, corner, gain, w_qkv, w_proj, table)
 
@@ -299,7 +300,7 @@
         out_specs=(spec,) * 3,
         scratch_shapes=[pltpu.SemaphoreType.DMA((2, 3)), pltpu.SemaphoreType.DMA((2, 3))],
         compiler_params=pltpu.CompilerParams(
-            collective_id=0, has_side_effects=True, vmem_limit_bytes=40 * 1024 * 1024
+            collective_id=0, has_side_effects=True, vmem_limit_bytes=8 * 1024 * 1024
         ),
         name="halo_in",
     )(air, up)
@@ -308,8 +309,8 @@
 def finish_kernel(
     lons, lats, air, up, out24, out8, grads, table,
     block_out, d_state, d_gain, d_wqkv, d_wproj, d_table,
-    got_n, got_e, got_c, land_w, land_t, land_lat, all_w, all_t,
-    h_send, h_recv, w_send, w_recv, t_send, t_recv, l_send, l_recv, gw_send, gw_recv, gt_send, gt_recv,
+    got_n, got_e, got_c, land_w, land_t, land_lat, all_w, all_t, land_g,
+    h_send, h_recv, w_send, w_recv, t_send, t_recv, l_send, l_recv, gw_send, gw_recv, gt_send, gt_recv, g_send, g_recv,
 ):
     me, me_lat = lax.axis_index("lon"), lax.axis_index("lat")
     rows, width = air.shape[1], air.shape[3]
@@ -323,7 +324,7 @@
     for k in range(1, lons):
         to = spot(k, 0)
         w_copies.append(remote(grads.at[to["lon"]], land_w.at[k - 1], w_send.at[k - 1], w_recv.at[k - 1], to))
-        t_copies.append(remote(table.at[to["lon"]], land_t.at[k - 1], t_send.at[k - 1], t_recv.at[k - 1], to))
+        t_copies.append(remote(table.at[to["lon"]], land_t.at[me], t_send.at[k - 1], t_recv.at[k - 1], to))
     rim = pl.ds(keep, LAT_SHIFT)
     own = pl.ds(0, keep)
     halos = [
@@ -346,10 +347,20 @@
     for copy in l_copies:
         copy.start()
 
-    total = table[me].astype(F32)
+    land_t[me] = table[me]
     for k in range(1, lons):
         t_copies[k - 1].wait_recv()
-        total = total + land_t[k - 1].astype(F32)
+    total = land_t[0].astype(F32)
+    for n in range(1, lons):
+        total = total + land_t[n].astype(F32)
+    t_share = table.shape[1]
+    land_g[me_lat] = total[t_share - 8:].astype(BF16)
+    g_copies = [
+        remote(land_g.at[me_lat], land_g.at[me_lat], g_send.at[k - 1], g_recv.at[k - 1], spot(0, k))
+        for k in range(1, lats)
+    ]
+    for copy in g_copies:
+        copy.start()
     all_t[me] = total.astype(BF16)
     gt_copies = [
         remote(all_t.at[me], all_t.at[me], gt_send.at[k - 1], gt_recv.at[k - 1], spot(k, 0))
@@ -385,20 +396,24 @@
     for copy in gw_copies:
         copy.start()
 
+    for copy in g_copies:
+        copy.wait_recv()
+    total = land_g[0].astype(F32)
+    for k in range(1, lats):
+        total = total + land_g[k].astype(F32)
+    d_gain[...] = total[:, 0:width]
     for copy in gt_copies:
         copy.wait_recv()
-    d_table[...] = all_t[...].astype(F32)
+    d_table[...] = all_t[:, 0:d_table.shape[1]].astype(F32)
     for copy in gw_copies:
         copy.wait_recv()
-    per = width // lons
-    d_wqkv[...] = all_w[:, 0:per, 0:3 * width].astype(F32)
-    d_wproj[...] = all_w[:, 0:per, 3 * width:4 * width].astype(F32)
-    d_gain[...] = all_w[0, per:per + 8, 0:width].astype(F32)
-    for copy in w_copies + t_copies + halos + l_copies + gt_copies + gw_copies:
+    d_wqkv[...] = all_w[:, :, 0:3 * width].astype(F32)
+    d_wproj[...] = all_w[:, :, 3 * width:4 * width].astype(F32)
+    for copy in w_copies + t_copies + halos + l_copies + gt_copies + gw_copies + g_copies:
         copy.wait_send()
 
 
-def finish_call(air, up, out24, out8, grads, table, lats):
+def finish_call(air, up, out24, out8, grads, table, lats, t_per):
     lev, rows, cols, width = air.shape
     lons, share, wide = grads.shape
     spec = pl.BlockSpec(memory_space=pltpu.VMEM)
@@ -412,7 +427,7 @@
             jax.ShapeDtypeStruct((8, width), F32),
             jax.ShapeDtypeStruct((lons, per, 3 * width), F32),
             jax.ShapeDtypeStruct((lons, per, width), F32),
-            jax.ShapeDtypeStruct(table.shape, F32),
+            jax.ShapeDtypeStruct((lons, t_per, table.shape[2]), F32),
         ),
         in_specs=[spec] * 6,
         out_specs=(spec,) * 6,
@@ -421,19 +436,21 @@
             pltpu.VMEM((2, lev, rows - LAT_SHIFT, EDGE, width), BF16),
             pltpu.VMEM((2, lev, LAT_SHIFT, EDGE, width), BF16),
             pltpu.VMEM((lons - 1, share, wide), BF16),
-            pltpu.VMEM((lons - 1,) + table.shape[1:], BF16),
+            pltpu.VMEM(table.shape, BF16),
             pltpu.VMEM((lats, share, wide), BF16),
             pltpu.VMEM(grads.shape, BF16),
             pltpu.VMEM(table.shape, BF16),
+            pltpu.VMEM((lats, 8, table.shape[2]), BF16),
             dma((3,)), dma((3,)),
             dma((lons - 1,)), dma((lons - 1,)),
             dma((lons - 1,)), dma((lons - 1,)),
             dma((lats - 1,)), dma((lats - 1,)),
             dma((lons - 1,)), dma((lons - 1,)),
             dma((lons - 1,)), dma((lons - 1,)),
+            dma((lats - 1,)), dma((lats - 1,)),
         ],
         compiler_params=pltpu.CompilerParams(
-            collective_id=1, has_side_effects=True, vmem_limit_bytes=40 * 1024 * 1024
+            collective_id=1, has_side_effects=True, vmem_limit_bytes=20 * 1024 * 1024
         ),
         name="finish",
     )(air, up, out24, out8, grads, table)
@@ -449,10 +466,10 @@
         bias_table.reshape(pairs * PLACES, PLACES * OFFS), lons,
     )
     block_out, d_state, d_gain, d_wqkv, d_wproj, d_table = finish_call(
-        air_state, upstream, out24, out8, grads, d_table, lats
+        air_state, upstream, out24, out8, grads, d_table, lats, pairs * PLACES // lons
     )
     return (
-        block_out, d_state, d_gain[0], d_wqkv.reshape(width, 3 * width), d_wproj.reshape(width, width),
+        block_out, d_state, d_gain[7], d_wqkv.reshape(width, 3 * width), d_wproj.reshape(width, width),
         d_table.reshape(bias_table.shape),
     )
 

time: 77.2 us -> 65.8 us (0.85)
  Pallas kernels: 64 us -> 58 us
  local copies, waits for them, and re-layouts: 12.2 us -> 6.97 us
    unnamed x28 -> x16, local copies, waits for them, and re-layouts: 10.6 us -> 6.07 us
    pallas_call x1, Pallas kernels: 24.1 us -> 19.6 us  [core_call(): pl.pallas_call(core_kernel, out_shape=(jax.ShapeDtypeStruct((2, lev, rows...]
    pallas_call x1, Pallas kernels: 24.8 us -> 23.4 us  [finish_call(): pl.pallas_call(partial(finish_kernel, lons, lats), out_shape=(jax.ShapeDt...]
where the time goes in v3:
time: 65.8 us; the launch traced here: 65.6 us
  Pallas kernels  58 us (88%)
  local copies, waits for them, and re-layouts  6.97 us (11%)
  between operations  0.72 us (1%)
    pallas_call x1, Pallas kernels, finish_call(): pl.pallas_call(partial(finish_kernel, lons, lats), out_shape=(jax.ShapeDt...  23.4 us
    pallas_call x1, Pallas kernels, core_call(): pl.pallas_call(core_kernel, out_shape=(jax.ShapeDtypeStruct((2, lev, rows...  19.6 us
    pallas_call x1, Pallas kernels, halo_call(): pl.pallas_call(halo_kernel, out_shape=(jax.ShapeDtypeStruct((2, lev, rows...  15 us
    unnamed x16, local copies, waits for them, and re-layouts  6.07 us

profile of v3, /device:TPU:0, one launch (start us, length us, event | category | flops | bytes accessed | tf_op | source)
XLA Modules:
  0.0 65.6 jit_solution(15458760910375439979)
XLA Ops:
  0.6 0.0 copy-start.1
  0.6 1.0 %copy.14 = f32[1,2,6,3312]{3,2,1,0:T(8,128)S(1)} copy(f32[1,2,6,3312]{3,1,2,0:T(2,128)} %param.11) | data formatting | bytes 317952 | tf_op args[5]
  1.6 0.0 copy-start
  1.6 0.2 reshape.28.table
  1.8 0.0 copy-done.1
  1.8 0.8 %copy-done = bf16[4,6,24,192]{3,2,1,0:T(8,128)(2,1)S(1)} copy-done((bf16[4,6,24,192]{3,2,1,0:T(8,128)(2,1)S(1)}, bf16[4,6,24,192]{3,2,1,0:T(8,128)(2,1)}, u32[]{:S(2)}) %copy-start) | copy-done | bytes 221208
  2.6 0.0 copy-start.2
  2.6 0.0 copy-start.3
  2.6 15.0 %halo_in.1 = (bf16[2,4,6,8,192]{4,3,2,1,0:T(8,128)(2,1)S(1)}, bf16[2,4,3,24,192]{4,3,2,1,0:T(8,128)(2,1)S(1)}, bf16[2,4,3,8,192]{4,3,2,1,0:T(8,128)(2,1)S(1)}) custom-call(bf16[4,6,24,192]{3,2,1,0:T(8,128)(2,1)S(1)} %copy-done, bf16[4,6,24,192]{3,2,1,0:T(8,128)(2,1)S(1)} %copy-done.1), custom_call_target="tpu_custom_call" | custom-call | tf_op jit(solution)/shard_map/halo_in/pallas_call | solution.py:292
  17.6 0.0 copy-start.4
  17.6 0.0 copy-done.2
  17.6 0.0 copy-done.3
  17.7 0.7 copy-done.4
  18.3 19.6 %window_core.1 = (bf16[2,4,6,24,192]{4,3,2,1,0:T(8,128)(2,1)S(1)}, bf16[2,4,6,8,192]{4,3,2,1,0:T(8,128)(2,1)S(1)}, bf16[8,24,768]{2,1,0:T(8,128)(2,1)S(1)}, bf16[8,24,276]{2,1,0:T(8,128)(2,1)S(1)}) custom-call(bf16[4,6,24,192]{3,2,1,0:T(8,128)(2,1)S(1)} %copy-done, bf16[4,6,24,192]{3,2,1,0:T(8,128)(2,1)S(1)} %copy-done.1, ...), custom_call_target="tpu_custom_call" | custom-call | tf_op jit(solution)/shard_map/window_core/pallas_call | solution.py:224
  37.9 23.4 %finish.1 = (bf16[4,6,24,192]{3,2,1,0:T(8,128)(2,1)S(1)}, bf16[4,6,24,192]{3,2,1,0:T(8,128)(2,1)S(1)}, f32[8,192]{1,0:T(8,128)S(1)}, f32[8,24,576]{2,1,0:T(8,128...) custom-call(bf16[4,6,24,192]{3,2,1,0:T(8,128)(2,1)S(1)} %copy-done, bf16[4,6,24,192]{3,2,1,0:T(8,128)(2,1)S(1)} %copy-done.1, ...), custom_call_target="tpu_custom_call" | custom-call | tf_op jit(solution)/shard_map/finish/pallas_call | solution.py:422
  61.3 0.6 slice.3
  61.8 0.2 reshape.31
  62.0 0.7 %copy.15 = f32[1,2,6,3312]{3,1,2,0:T(2,128)} copy(f32[1,2,6,3312]{3,2,1,0:T(8,128)S(1)} %reshape.31) | data formatting | bytes 317952
  62.8 0.7 %copy.20 = bf16[4,6,24,192]{3,2,1,0:T(8,128)(2,1)} copy(bf16[4,6,24,192]{3,2,1,0:T(8,128)(2,1)S(1)} %get-tuple-element.50) | data formatting | bytes 442368
  63.5 0.7 %copy.21 = bf16[4,6,24,192]{3,2,1,0:T(8,128)(2,1)} copy(bf16[4,6,24,192]{3,2,1,0:T(8,128)(2,1)S(1)} %get-tuple-element.51) | data formatting | bytes 442368
  64.2 0.8 %copy.22 = f32[192,576]{1,0:T(8,128)} copy(f32[192,576]{1,0:T(8,128)S(1)} %bitcast.4) | data formatting | bytes 884736
  65.0 0.7 %copy.23 = f32[192,192]{1,0:T(8,128)} copy(f32[192,192]{1,0:T(8,128)S(1)} %bitcast.5) | data formatting | bytes 294912
Async XLA Ops:
  0.6 1.2 %copy-start.1 = (bf16[4,6,24,192]{3,2,1,0:T(8,128)(2,1)S(1)}, bf16[4,6,24,192]{3,2,1,0:T(8,128)(2,1)}, u32[]{:S(2)}) copy-start(bf16[4,6,24,192]{3,2,1,0:T(8,128)(2,1)} %up.5) | copy-start | bytes 663556
  1.6 1.0 %copy-start = (bf16[4,6,24,192]{3,2,1,0:T(8,128)(2,1)S(1)}, bf16[4,6,24,192]{3,2,1,0:T(8,128)(2,1)}, u32[]{:S(2)}) copy-start(bf16[4,6,24,192]{3,2,1,0:T(8,128)(2,1)} %air.5) | copy-start | bytes 663556
  2.6 15.0 %copy-start.2 = (bf16[192,576]{1,0:T(8,128)(2,1)S(1)}, bf16[192,576]{1,0:T(8,128)(2,1)}, u32[]{:S(2)}) copy-start(bf16[192,576]{1,0:T(8,128)(2,1)} %w_qkv.1) | copy-start | bytes 663556
  2.6 15.0 %copy-start.3 = (bf16[192,192]{1,0:T(8,128)(2,1)S(1)}, bf16[192,192]{1,0:T(8,128)(2,1)}, u32[]{:S(2)}) copy-start(bf16[192,192]{1,0:T(8,128)(2,1)} %w_proj.1) | copy-start | bytes 221188
  17.6 0.7 %copy-start.4 = (f32[192]{0:T(256)S(1)}, f32[192]{0:T(256)}, u32[]{:S(2)}) copy-start(f32[192]{0:T(256)} %param.8) | copy-start | bytes 2308

commit v4 on v3

--- a/solution.py
+++ b/solution.py
@@ -48,9 +48,9 @@
 
 
 def core_kernel(
-    air, up, east, north, corner, gain, w_qkv, w_proj, table,
+    air, up, east, north, corner, gain, w_qkv, w_proj, bias,
     out24, out8, grads, d_table,
-    x, y, xhat, rstd_s, normed, qkv, d_mix, bias, d_bias, acc_o, acc_dq, acc_dk, acc_dv, dqkv, mix, stage,
+    x, y, xhat, rstd_s, normed, qkv, d_mix, d_bias, acc_o, acc_dq, acc_dk, acc_dv, dqkv, mix, stage,
 ):
     lev, rows, cols, width = air.shape
     lev_wins, lon_wins = lev // WLEV, cols // WLON
@@ -80,17 +80,7 @@
                         dst[w, p * WLON:p * WLON + WLON - LON_SHIFT, :] = row[lo:cols]
                         dst[w, p * WLON + WLON - LON_SHIFT:(p + 1) * WLON, :] = edge[:LON_SHIFT]
 
-    t_val = table[...]
-    t_hi = t_val.astype(BF16)
-    t_rest = t_val - t_hi.astype(F32)
-    t_mid = t_rest.astype(BF16)
-    t_lo = (t_rest - t_mid.astype(F32)).astype(BF16)
     last_band = lax.axis_index("lat") == lax.axis_size("lat") - 1
-    for lon_i in range(WLON):
-        sel = selection(lon_i)
-        b = mm(t_hi, sel) + mm(t_mid, sel) + mm(t_lo, sel)
-        bias[:, lon_i, :] = b
-
     wq_all = w_qkv[...]
     for w in range(wins):
         xv = x[w]
@@ -160,7 +150,7 @@
         d_bias[pl.ds(ah * PLACES, PLACES)] = d_bias_h.reshape(PLACES, WLON, WIN)
         return carry
 
-    lax.fori_loop(0, lev_wins * HEADS, head_step, 0, unroll=2)
+    lax.fori_loop(0, lev_wins * HEADS, head_step, 0, unroll=4)
 
     total = None
     for lon_i in range(WLON):
@@ -212,11 +202,11 @@
         d_table[n] = rows_n.astype(BF16)
 
 
-def core_call(air, up, east, north, corner, gain, w_qkv, w_proj, table, parts):
+def core_call(air, up, east, north, corner, gain, w_qkv, w_proj, bias, parts):
     lev, rows, cols, width = air.shape
     wins = (lev // WLEV) * (cols // WLON)
     pairs = (lev // WLEV) * HEADS
-    t_share = table.shape[0] // parts // 8 * 8 + 8
+    t_share = pairs * PLACES // parts // 8 * 8 + 8
     vm = lambda shape, dtype: pltpu.VMEM(shape, dtype)
     win_f = vm((wins, WIN, width), F32)
     win_b = vm((wins, WIN, width), BF16)
@@ -227,7 +217,7 @@
             jax.ShapeDtypeStruct((2, lev, rows, cols, width), BF16),
             jax.ShapeDtypeStruct((2, lev, rows, EDGE, width), BF16),
             jax.ShapeDtypeStruct((parts, width // parts, 4 * width), BF16),
-            jax.ShapeDtypeStruct((parts, t_share, table.shape[1]), BF16),
+            jax.ShapeDtypeStruct((parts, t_share, PLACES * OFFS), BF16),
         ),
         in_specs=[spec] * 9,
         out_specs=(spec,) * 4,
@@ -238,7 +228,6 @@
             vm((3, wins, WIN, width), BF16),
             win_b,
             vm((pairs * PLACES, WLON, WIN), F32),
-            vm((pairs * PLACES, WLON, WIN), F32),
             win_f, win_f, win_f, win_f,
             vm((wins, WIN, 3 * width), BF16),
             win_b,
@@ -246,7 +235,7 @@
         ],
         compiler_params=pltpu.CompilerParams(vmem_limit_bytes=26 * 1024 * 1024),
         name="window_core",
-    )(air, up, east, north, corner, gain, w_qkv, w_proj, table)
+    )(air, up, east, north, corner, gain, w_qkv, w_proj, bias)
 
 
 def spot(lon=0, lat=0):
@@ -269,7 +258,7 @@
     )
 
 
-def halo_kernel(air, up, east, north, corner, send, recv):
+def halo_kernel(air, up, table, east, north, corner, bias, send, recv):
     greet([spot(-1, 0), spot(0, -1), spot(-1, -1), spot(1, 0), spot(0, 1), spot(1, 1)])
     copies = []
     for n, src in enumerate((air, up)):
@@ -282,11 +271,20 @@
         ]
     for copy in copies:
         copy.start()
+    t_val = table[...]
+    t_hi = t_val.astype(BF16)
+    t_rest = t_val - t_hi.astype(F32)
+    t_mid = t_rest.astype(BF16)
+    t_lo = (t_rest - t_mid.astype(F32)).astype(BF16)
+    for lon_i in range(WLON):
+        sel = selection(lon_i)
+        b = mm(t_hi, sel) + mm(t_mid, sel) + mm(t_lo, sel)
+        bias[:, lon_i, :] = b
     for copy in copies:
         copy.wait()
 
 
-def halo_call(air, up):
+def halo_call(air, up, table):
     lev, rows, cols, width = air.shape
     spec = pl.BlockSpec(memory_space=pltpu.VMEM)
     return pl.pallas_call(
@@ -295,15 +293,16 @@
             jax.ShapeDtypeStruct((2, lev, rows, EDGE, width), BF16),
             jax.ShapeDtypeStruct((2, lev, LAT_SHIFT, cols, width), BF16),
             jax.ShapeDtypeStruct((2, lev, LAT_SHIFT, EDGE, width), BF16),
-        ),
-        in_specs=[spec] * 2,
-        out_specs=(spec,) * 3,
+            jax.ShapeDtypeStruct((table.shape[0], WLON, WIN), F32),
+        ),
+        in_specs=[spec] * 3,
+        out_specs=(spec,) * 4,
         scratch_shapes=[pltpu.SemaphoreType.DMA((2, 3)), pltpu.SemaphoreType.DMA((2, 3))],
         compiler_params=pltpu.CompilerParams(
-            collective_id=0, has_side_effects=True, vmem_limit_bytes=8 * 1024 * 1024
+            collective_id=0, has_side_effects=True, vmem_limit_bytes=16 * 1024 * 1024
         ),
         name="halo_in",
-    )(air, up)
+    )(air, up, table)
 
 
 def finish_kernel(
@@ -460,10 +459,11 @@
     lev, rows, cols, width = air_state.shape
     lons, lats = lax.axis_size("lon"), lax.axis_size("lat")
     pairs = (lev // WLEV) * HEADS
-    east, north, corner = halo_call(air_state, upstream)
+    table = bias_table.reshape(pairs * PLACES, PLACES * OFFS)
+    east, north, corner, bias = halo_call(air_state, upstream, table)
     out24, out8, grads, d_table = core_call(
         air_state, upstream, east, north, corner, norm_gain.reshape(1, width), w_qkv, w_proj,
-        bias_table.reshape(pairs * PLACES, PLACES * OFFS), lons,
+        bias, lons,
     )
     block_out, d_state, d_gain, d_wqkv, d_wproj, d_table = finish_call(
         air_state, upstream, out24, out8, grads, d_table, lats, pairs * PLACES // lons

time: 65.8 us -> 67.4 us (1.024)
  local copies, waits for them, and re-layouts: 6.97 us -> 11.8 us
  Pallas kernels: 58 us -> 54.6 us
    unnamed x16 -> x20, local copies, waits for them, and re-layouts: 6.07 us -> 10.9 us
    pallas_call x1, Pallas kernels: 19.6 us -> 16.2 us  [core_call(): pl.pallas_call(core_kernel, out_shape=(jax.ShapeDtypeStruct((2, lev, rows...]
where the time goes in v4:
time: 67.4 us; the launch traced here: 67.1 us
  Pallas kernels  54.6 us (81%)
  local copies, waits for them, and re-layouts  11.8 us (18%)
  between operations  0.69 us (1%)
    pallas_call x1, Pallas kernels, finish_call(): pl.pallas_call(partial(finish_kernel, lons, lats), out_shape=(jax.ShapeDt...  23.4 us
    pallas_call x1, Pallas kernels, core_call(): pl.pallas_call(core_kernel, out_shape=(jax.ShapeDtypeStruct((2, lev, rows...  16.2 us
    pallas_call x1, Pallas kernels, halo_call(): pl.pallas_call(halo_kernel, out_shape=(jax.ShapeDtypeStruct((2, lev, rows...  15 us
    unnamed x20, local copies, waits for them, and re-layouts  10.9 us

profile of v4, /device:TPU:0, one launch (start us, length us, event | category | flops | bytes accessed | tf_op | source)
XLA Modules:
  0.0 67.1 jit_solution(14609252222530145090)
XLA Ops:
  0.6 0.9 %copy.14 = f32[1,2,6,3312]{3,2,1,0:T(8,128)S(1)} copy(f32[1,2,6,3312]{3,1,2,0:T(2,128)} %param.11) | data formatting | bytes 317952 | tf_op args[5]
  1.6 0.2 reshape.27.table
  1.7 0.0 copy-start
  1.8 1.0 %copy-done = bf16[4,6,24,192]{3,2,1,0:T(8,128)(2,1)S(1)} copy-done((bf16[4,6,24,192]{3,2,1,0:T(8,128)(2,1)S(1)}, bf16[4,6,24,192]{3,2,1,0:T(8,128)(2,1)}, u32[]{:S(2)}) %copy-start) | copy-done | bytes 221208
  2.7 0.0 copy-start.2
  2.7 1.0 %copy-done.2 = bf16[4,6,24,192]{3,2,1,0:T(8,128)(2,1)S(1)} copy-done((bf16[4,6,24,192]{3,2,1,0:T(8,128)(2,1)S(1)}, bf16[4,6,24,192]{3,2,1,0:T(8,128)(2,1)}, u32[]{:S(2)}) %copy-start.2) | copy-done | bytes 221208
  3.7 15.0 %halo_in.1 = (bf16[2,4,6,8,192]{4,3,2,1,0:T(8,128)(2,1)S(1)}, bf16[2,4,3,24,192]{4,3,2,1,0:T(8,128)(2,1)S(1)}, bf16[2,4,3,8,192]{4,3,2,1,0:T(8,128)(2,1)S(1)}, f32[144,12,144]{2,1,0:T(8,128)S(1)}) custom-call(bf16[4,6,24,192]{3,2,1,0:T(8,128)(2,1)S(1)} %copy-done, bf16[4,6,24,192]{3,2,1,0:T(8,128)(2,1)S(1)} %copy-done.2, f32[144,276]{1,0:T(8,128)S(1)} %reshape.27.table), custom_call_target="tpu_custom_call" | custom-call | tf_op jit(solution)/shard_map/halo_in/pallas_call | solution.py:290
  18.7 0.0 copy-start.1
  18.7 1.0 %copy-done.1 = bf16[4,6,24,192]{3,2,1,0:T(8,128)(2,1)S(1)} copy-done((bf16[4,6,24,192]{3,2,1,0:T(8,128)(2,1)S(1)}, bf16[4,6,24,192]{3,2,1,0:T(8,128)(2,1)}, u32[]{:S(2)}) %copy-start.1) | copy-done | bytes 221208
  19.7 0.0 copy-start.3
  19.7 1.0 %copy-done.3 = bf16[4,6,24,192]{3,2,1,0:T(8,128)(2,1)S(1)} copy-done((bf16[4,6,24,192]{3,2,1,0:T(8,128)(2,1)S(1)}, bf16[4,6,24,192]{3,2,1,0:T(8,128)(2,1)}, u32[]{:S(2)}) %copy-start.3) | copy-done | bytes 221208
  20.6 0.0 copy-start.4
  20.6 0.9 %copy-done.4 = bf16[192,576]{1,0:T(8,128)(2,1)S(1)} copy-done((bf16[192,576]{1,0:T(8,128)(2,1)S(1)}, bf16[192,576]{1,0:T(8,128)(2,1)}, u32[]{:S(2)}) %copy-start.4) | copy-done | bytes 221208
  21.6 0.0 copy-start.5
  21.6 0.9 %copy-done.5 = bf16[192,192]{1,0:T(8,128)(2,1)S(1)} copy-done((bf16[192,192]{1,0:T(8,128)(2,1)S(1)}, bf16[192,192]{1,0:T(8,128)(2,1)}, u32[]{:S(2)}) %copy-start.5) | copy-done | bytes 73752
  22.5 0.0 copy-start.6
  22.5 0.7 %copy-done.6 = f32[192]{0:T(256)S(1)} copy-done((f32[192]{0:T(256)S(1)}, f32[192]{0:T(256)}, u32[]{:S(2)}) %copy-start.6) | copy-done | bytes 792
  23.1 16.2 %window_core.1 = (bf16[2,4,6,24,192]{4,3,2,1,0:T(8,128)(2,1)S(1)}, bf16[2,4,6,8,192]{4,3,2,1,0:T(8,128)(2,1)S(1)}, bf16[8,24,768]{2,1,0:T(8,128)(2,1)S(1)}, bf16[8,24,276]{2,1,0:T(8,128)(2,1)S(1)}) custom-call(bf16[4,6,24,192]{3,2,1,0:T(8,128)(2,1)S(1)} %copy-done.1, bf16[4,6,24,192]{3,2,1,0:T(8,128)(2,1)S(1)} %copy-done.3, ...), custom_call_target="tpu_custom_call" | custom-call | tf_op jit(solution)/shard_map/window_core/pallas_call | solution.py:214
  39.3 23.4 %finish.1 = (bf16[4,6,24,192]{3,2,1,0:T(8,128)(2,1)S(1)}, bf16[4,6,24,192]{3,2,1,0:T(8,128)(2,1)S(1)}, f32[8,192]{1,0:T(8,128)S(1)}, f32[8,24,576]{2,1,0:T(8,128...) custom-call(bf16[4,6,24,192]{3,2,1,0:T(8,128)(2,1)S(1)} %copy-done.1, bf16[4,6,24,192]{3,2,1,0:T(8,128)(2,1)S(1)} %copy-done.3, ...), custom_call_target="tpu_custom_call" | custom-call | tf_op jit(solution)/shard_map/finish/pallas_call | solution.py:421
  62.7 0.6 slice.3
  63.3 0.2 reshape.31
  63.5 0.7 %copy.15 = f32[1,2,6,3312]{3,1,2,0:T(2,128)} copy(f32[1,2,6,3312]{3,2,1,0:T(8,128)S(1)} %reshape.31) | data formatting | bytes 317952
  64.2 0.7 %copy.20 = bf16[4,6,24,192]{3,2,1,0:T(8,128)(2,1)} copy(bf16[4,6,24,192]{3,2,1,0:T(8,128)(2,1)S(1)} %get-tuple-element.52) | data formatting | bytes 442368
  64.9 0.7 %copy.21 = bf16[4,6,24,192]{3,2,1,0:T(8,128)(2,1)} copy(bf16[4,6,24,192]{3,2,1,0:T(8,128)(2,1)S(1)} %get-tuple-element.53) | data formatting | bytes 442368
  65.6 0.8 %copy.22 = f32[192,576]{1,0:T(8,128)} copy(f32[192,576]{1,0:T(8,128)S(1)} %bitcast.4) | data formatting | bytes 884736
  66.4 0.7 %copy.23 = f32[192,192]{1,0:T(8,128)} copy(f32[192,192]{1,0:T(8,128)S(1)} %bitcast.5) | data formatting | bytes 294912
Async XLA Ops:
  1.7 1.0 %copy-start = (bf16[4,6,24,192]{3,2,1,0:T(8,128)(2,1)S(1)}, bf16[4,6,24,192]{3,2,1,0:T(8,128)(2,1)}, u32[]{:S(2)}) copy-start(bf16[4,6,24,192]{3,2,1,0:T(8,128)(2,1)} %air.5) | copy-start | bytes 663556
  2.7 1.0 %copy-start.2 = (bf16[4,6,24,192]{3,2,1,0:T(8,128)(2,1)S(1)}, bf16[4,6,24,192]{3,2,1,0:T(8,128)(2,1)}, u32[]{:S(2)}) copy-start(bf16[4,6,24,192]{3,2,1,0:T(8,128)(2,1)} %up.5) | copy-start | bytes 663556
  18.7 1.0 %copy-start.1 = (bf16[4,6,24,192]{3,2,1,0:T(8,128)(2,1)S(1)}, bf16[4,6,24,192]{3,2,1,0:T(8,128)(2,1)}, u32[]{:S(2)}) copy-start(bf16[4,6,24,192]{3,2,1,0:T(8,128)(2,1)} %air.5) | copy-start | bytes 663556
  19.7 1.0 %copy-start.3 = (bf16[4,6,24,192]{3,2,1,0:T(8,128)(2,1)S(1)}, bf16[4,6,24,192]{3,2,1,0:T(8,128)(2,1)}, u32[]{:S(2)}) copy-start(bf16[4,6,24,192]{3,2,1,0:T(8,128)(2,1)} %up.5) | copy-start | bytes 663556
  20.6 0.9 %copy-start.4 = (bf16[192,576]{1,0:T(8,128)(2,1)S(1)}, bf16[192,576]{1,0:T(8,128)(2,1)}, u32[]{:S(2)}) copy-start(bf16[192,576]{1,0:T(8,128)(2,1)} %w_qkv.1) | copy-start | bytes 663556
  21.6 0.9 %copy-start.5 = (bf16[192,192]{1,0:T(8,128)(2,1)S(1)}, bf16[192,192]{1,0:T(8,128)(2,1)}, u32[]{:S(2)}) copy-start(bf16[192,192]{1,0:T(8,128)(2,1)} %w_proj.1) | copy-start | bytes 221188
  22.5 0.7 %copy-start.6 = (f32[192]{0:T(256)S(1)}, f32[192]{0:T(256)}, u32[]{:S(2)}) copy-start(f32[192]{0:T(256)} %param.8) | copy-start | bytes 2308
